TPU v7x, 512 devices: a whole 4x4x16 slice. The times are simulated.
512 devices in a mesh: band: 64 (over z, x), member: 8 (over y, core).
Axes of the slice: x: 4, y: 4, z: 16, core: 2. Of those that a mesh axis runs over, the one named last changes fastest.
Arguments:
- scaled_atmosphere_field: float32 [80, 16384], P(None, 'band'), may hold values from -6 to 6
- perturbation: bfloat16 [8, 80, 16384], P('member', None, 'band'), may hold values from -6 to 6
- target: bfloat16 [8, 80, 16384], P('member', None, 'band'), may hold values from -6 to 6
- weight_map: bfloat16 [80, 16384], P(None, 'band'), may hold values from 0.01 to 10
- enc_send: int32 [64, 64, 8], P('band'), may hold values from -1 to 255, as said below
- enc_recv: int32 [64, 64, 8], P('band'), may hold values from -1 to 255, as said below
- dec_send: int32 [64, 64, 8], P('band'), may hold values from -1 to 255, as said below
- dec_recv: int32 [64, 64, 8], P('band'), may hold values from -1 to 255, as said below
- lattice_lift_matrix: bfloat16 [80, 512], replicated, may hold values from -0.625 to 0.625
- mixing_rescale_factor: float32 [512], replicated, may hold values from 0.1 to 1.9
- expand_matrix: bfloat16 [512, 512], replicated, may hold values from -0.25 to 0.25
- contract_matrix: bfloat16 [512, 512], replicated, may hold values from -0.25 to 0.25
- readout_matrix: bfloat16 [512, 80], replicated, may hold values from -0.25 to 0.25
Outputs:
- student_outputs: float32 [8, 80, 16384], P('member', None, 'band')
- mesh_grad: bfloat16 [8, 16384, 512], P('member', 'band')
- grad_up: float32 [8, 512, 512], P('member')
- grad_down: float32 [8, 512, 512], P('member')
- grad_dec: float32 [8, 512, 80], P('member')
- grad_gain: float32 [8, 512], P('member')
Inputs may be any that keep to these rules, and one draw needn't show every extreme that they name: enc_send[s, d, k] is a local grid cell of band s (0 to 255) or -1 for an empty slot; in every draw one band fills all its slots and one partition receives full blocks of 8 from every band. enc_recv[d, s, k] is a local mesh node of partition d, and -1 exactly where enc_send[s, d, k] is -1. dec_send[s, d, k] is a local mesh node of partition s or -1 for an empty slot; in every draw one partition fills all its slots and one band receives full blocks of 8 from every partition. dec_recv[d, s, k] is a local grid cell of band d, and -1 exactly where dec_send[s, d, k] is -1.
All inputs are finite; a program needn't handle non-finite values.
Results may differ from a plain program's by a relative error of at most 0.0062.
Values may be sent and summed in bfloat16 or wider, within the bound.
A program may use at most 64 MiB of HBM per device.

v0:
```python
import math

import jax
import jax.numpy as jnp
from jax import lax
from jax.sharding import PartitionSpec as P

MESH_DEV = 256


smooth_sq = 0.01
norm_eps = 1e-05


def sent_to_all(array, axis):
    size = lax.axis_size(axis)
    return lax.all_to_all(
        jnp.broadcast_to(array[None], (size, *array.shape)), axis, 0, 0, tiled=True
    )


def in_order(tiles, dim):
    lengths = list(tiles.shape[1:])
    lengths[dim] *= tiles.shape[0]
    return jnp.moveaxis(tiles, 0, dim).reshape(lengths)


def gather_directly(array, axis, dim):
    tiles = sent_to_all(array, axis)
    return in_order(tiles, dim)


def sent_together(arrays, axis, dim, along):
    ends, at = ([], 0)
    for a in arrays[:-1]:
        at += a.shape[along]
        ends.append(at)
    both = jnp.concatenate(arrays, axis=along)
    return tuple(jnp.split(gather_directly(both, axis, dim), ends, axis=along))


def slope(diff):
    return diff * lax.rsqrt(diff * diff + smooth_sq)


def embed_columns(columns, lattice_lift_matrix):
    pre_act = lax.dot_general(
        columns, lattice_lift_matrix, (((0,), (0,)), ((), ())), preferred_element_type=jnp.float32
    )
    return jax.nn.silu(pre_act).astype(jnp.bfloat16)


def body(
    scaled_atmosphere_field,
    perturbation,
    target,
    weight_map,
    enc_send,
    enc_recv,
    dec_send,
    dec_recv,
    lattice_lift_matrix,
    mixing_rescale_factor,
    expand_matrix,
    contract_matrix,
    readout_matrix,
):
    highest = lax.Precision.HIGHEST
    band_count = lax.axis_size("band")
    channels, grid_rows = scaled_atmosphere_field.shape
    node_rows = MESH_DEV
    enc_width = enc_send.shape[2]
    dec_width = dec_send.shape[2]
    cell_ids = jnp.arange(grid_rows, dtype=jnp.int32)
    node_ids = jnp.arange(node_rows, dtype=jnp.int32)
    inputs_b = (scaled_atmosphere_field + perturbation[0].astype(jnp.float32)).astype(jnp.bfloat16)
    send_index = enc_send[0].reshape(-1)
    picker = (send_index[:, None] == cell_ids[None, :]).astype(jnp.bfloat16)
    picked = lax.dot_general(
        inputs_b, picker, (((1,), (1,)), ((), ())), preferred_element_type=jnp.float32
    ).astype(jnp.bfloat16)
    arrived = lax.all_to_all(
        picked.reshape(channels, band_count, enc_width),
        "band",
        split_axis=1,
        concat_axis=1,
        tiled=True,
    )
    slot_rows = embed_columns(arrived.reshape(channels, -1), lattice_lift_matrix)
    recv_index = enc_recv[0].reshape(-1)
    landing = (node_ids[:, None] == recv_index[None, :]).astype(jnp.bfloat16)
    summed = jnp.dot(landing, slot_rows, preferred_element_type=jnp.float32)
    edge_count = jnp.sum(landing.astype(jnp.float32), axis=1, keepdims=True)
    mesh_state = summed / jnp.maximum(edge_count, 1.0)
    recip = lax.rsqrt(jnp.mean(mesh_state * mesh_state, axis=1, keepdims=True) + norm_eps)
    normed_b = (mesh_state * recip * mixing_rescale_factor).astype(jnp.bfloat16)
    hidden_pre = jnp.dot(normed_b, expand_matrix, preferred_element_type=jnp.float32)
    hidden_b = jax.nn.silu(hidden_pre).astype(jnp.bfloat16)
    mesh_next = mesh_state + jnp.dot(hidden_b, contract_matrix, preferred_element_type=jnp.float32)
    next_b = mesh_next.astype(jnp.bfloat16)
    dec_index = dec_send[0].reshape(-1)
    mesh_picker = (dec_index[:, None] == node_ids[None, :]).astype(jnp.bfloat16)
    cell_index = dec_recv[0].reshape(-1)
    fill_map = (cell_ids[:, None] == cell_index[None, :]).astype(jnp.bfloat16)
    grid_count = jnp.sum(fill_map.astype(jnp.float32), axis=1)
    inverse = 1.0 / jnp.maximum(grid_count, 1.0)
    projected = lax.dot_general(
        readout_matrix, next_b, (((0,), (1,)), ((), ())), preferred_element_type=jnp.float32
    ).astype(jnp.bfloat16)
    chosen = lax.dot_general(
        projected, mesh_picker, (((1,), (1,)), ((), ())), preferred_element_type=jnp.float32
    ).astype(jnp.bfloat16)
    slot_values = lax.all_to_all(
        chosen.reshape(channels, band_count, dec_width),
        "band",
        split_axis=1,
        concat_axis=1,
        tiled=True,
    ).reshape(channels, -1)
    grid_sum = lax.dot_general(
        slot_values, fill_map, (((1,), (1,)), ((), ())), preferred_element_type=jnp.float32
    )
    student_outputs = scaled_atmosphere_field + grid_sum * inverse[None, :]
    all_pred, all_target = sent_together(
        (student_outputs[None], target.astype(jnp.float32)), "member", 0, 1
    )
    teacher_terms = jnp.sum(slope(student_outputs[None] - all_target), axis=0)
    own_terms = jnp.sum(slope(student_outputs[None] - all_pred), axis=0)
    pred_grad = weight_map.astype(jnp.float32) * (teacher_terms - own_terms)
    scaled = pred_grad * inverse[None, :]
    slot_grad = jnp.dot(scaled, fill_map.astype(jnp.float32), precision=highest)
    dec_f32 = readout_matrix.astype(jnp.float32)
    picker_f32 = mesh_picker.astype(jnp.float32)
    returned = lax.all_to_all(
        slot_grad.reshape(channels, band_count, dec_width),
        "band",
        split_axis=1,
        concat_axis=1,
        tiled=True,
    ).reshape(channels, -1)
    node_grad = jnp.dot(returned, picker_f32, precision=highest)
    next_grad = lax.dot_general(node_grad, dec_f32, (((0,), (1,)), ((), ())), precision=highest)
    dec_part = lax.dot_general(
        next_b.astype(jnp.float32), node_grad, (((0,), (1,)), ((), ())), precision=highest
    )
    down_part = lax.dot_general(
        hidden_b.astype(jnp.float32), next_grad, (((0,), (0,)), ((), ())), precision=highest
    )
    hidden_grad = lax.dot_general(
        next_grad, contract_matrix.astype(jnp.float32), (((1,), (1,)), ((), ())), precision=highest
    )
    sigma = jax.nn.sigmoid(hidden_pre)
    pre_grad = hidden_grad * sigma * (1.0 + hidden_pre * (1.0 - sigma))
    up_part = lax.dot_general(
        normed_b.astype(jnp.float32), pre_grad, (((0,), (0,)), ((), ())), precision=highest
    )
    normed_grad = lax.dot_general(
        pre_grad, expand_matrix.astype(jnp.float32), (((1,), (1,)), ((), ())), precision=highest
    )
    gain_part = jnp.sum(normed_grad * mesh_state * recip, axis=0)
    gained = normed_grad * mixing_rescale_factor
    state_grad = (
        next_grad
        + recip * gained
        - mesh_state
        * (recip * recip * recip)
        * jnp.mean(gained * mesh_state, axis=1, keepdims=True)
    )
    up_sum, down_sum, dec_sum, gain_sum = lax.psum(
        (up_part, down_part, dec_part, gain_part), "band"
    )
    factor = 1.0 / math.sqrt(band_count * node_rows)
    return (
        student_outputs[None],
        state_grad.astype(jnp.bfloat16)[None],
        (up_sum * factor)[None],
        (down_sum * factor)[None],
        (dec_sum * factor)[None],
        (gain_sum * factor)[None],
    )


def solution(mesh):
    return jax.shard_map(
        body,
        mesh=mesh,
        in_specs=(
            P(None, "band"),
            P("member", None, "band"),
            P("member", None, "band"),
            P(None, "band"),
            P("band", None, None),
            P("band", None, None),
            P("band", None, None),
            P("band", None, None),
            P(),
            P(),
            P(),
            P(),
            P(),
        ),
        out_specs=(
            P("member", None, "band"),
            P("member", "band", None),
            P("member", None, None),
            P("member", None, None),
            P("member", None, None),
            P("member", None),
        ),
        check_vma=False,
    )
```

profile of v0, /device:TPU:8, one launch (start us, length us, event | category | flops | bytes accessed | tf_op | source)
XLA Modules:
  0.0 412.4 jit_solution(2827426839130598299)
XLA Ops:
  7.2 0.0 copy-start
  7.2 0.8 copy.34
  8.0 0.1 eq.64
  8.1 1.2 convolution_convert_fusion.1
  9.3 0.8 copy.35
  10.0 18.6 %all-to-all-start = ((bf16[80,64,8]{0,2,1:T(8,128)(2,1)}), bf16[80,64,8]{0,2,1:T(8,128)(2,1)S(1)}, u32[]{:S(2)}, u32[]{:S(2)}) async-start(bf16[80,64,8]{0,2,1:T(8,128)(2,1)} %bitcast.1), calls=%async_computation | async-start | bytes 262144 | tf_op jit(solution)/shard_map/all_to_all | solution.py:82
  28.6 0.8 copy.33
  29.4 0.1 eq.61
  29.5 0.8 copy.36
  30.3 0.1 eq.68
  30.3 0.8 copy.38
  31.1 0.1 eq.73
  31.2 0.8 convert_element_type.77
  32.0 0.1 convert_reduce_fusion.1
  32.1 0.0 copy-start.4
  32.2 14.1 %all-to-all-done = bf16[80,64,8]{0,2,1:T(8,128)(2,1)S(1)} async-done(((bf16[80,64,8]{0,2,1:T(8,128)(2,1)}), bf16[80,64,8]{0,2,1:T(8,128)(2,1)S(1)}, u32[]{:S(2)}, u32[]{:S(2)}) %all-to-all-start) | async-done | bytes 81952 | tf_op jit(solution)/shard_map/all_to_all | solution.py:82
  46.3 1.6 multiply_reduce_fusion.4
  48.0 0.3 fusion.28
  48.3 0.7 copy-done.5
  49.0 0.3 fusion.1
  49.3 0.5 copy-done.2
  49.9 0.5 convolution_convert_fusion
  50.3 0.8 copy.37
  51.1 4.6 %all-to-all-start.1 = ((bf16[80,64,8]{0,2,1:T(8,128)(2,1)}), bf16[80,64,8]{0,2,1:T(8,128)(2,1)S(1)}, u32[]{:S(2)}, u32[]{:S(2)}) async-start(bf16[80,64,8]{0,2,1:T(8,128)(2,1)} %bitcast.3), calls=%async_computation.1 | async-start | bytes 262144 | tf_op jit(solution)/shard_map/all_to_all | solution.py:113
  55.7 0.0 all-reduce.3.cloned.1.call-start
  55.7 0.1 convert_reduce_fusion
  55.9 16.6 %all-to-all-done.1 = bf16[80,64,8]{0,2,1:T(8,128)(2,1)S(1)} async-done(((bf16[80,64,8]{0,2,1:T(8,128)(2,1)}), bf16[80,64,8]{0,2,1:T(8,128)(2,1)S(1)}, u32[]{:S(2)}, u32[]{:S(2)}) %all-to-all-start.1) | async-done | bytes 81952 | tf_op jit(solution)/shard_map/all_to_all | solution.py:113
  72.5 0.2 fusion.2
  72.7 0.1 broadcast_in_dim.18
  72.9 22.2 %all_to_all.20 = f32[8,1,160,256]{3,2,1,0:T(8,128)S(1)} all-to-all(f32[8,1,160,256]{3,2,1,0:T(8,128)S(1)} %broadcast_in_dim.18), channel_id=1, replica_groups=mesh['band'=64,'member'=8] {'member'}, dimensions={0} | all-to-all | bytes 2621440 | tf_op jit(solution)/shard_map/all_to_all | solution.py:17
  95.0 0.3 multiply_reduce_fusion
  95.3 0.5 copy-done.3
  95.8 0.6 convolution_bitcast_fusion
  96.4 26.3 %all_to_all.21 = f32[80,64,8]{0,2,1:T(8,128)S(1)} all-to-all(f32[80,64,8]{0,2,1:T(8,128)S(1)} %convolution_bitcast_fusion), channel_id=1, replica_groups=mesh['band'=64,'member'=8] {'band'}, dimensions={1} | all-to-all | bytes 327680 | tf_op jit(solution)/shard_map/all_to_all | solution.py:134
  122.7 0.5 fusion.4
  123.2 0.9 fusion.33
  124.1 0.4 fusion.32
  124.6 0.7 fusion
  125.3 1.7 fusion.29
  126.9 1.7 fusion.27
  128.7 0.0 all-reduce.3.cloned.1.call-update
  128.7 0.7 multiply_reduce_fusion.2
  129.4 139.1 %psum.31 = f32[512]{0:T(512)S(1)} all-reduce(f32[512]{0:T(512)S(1)} %get-tuple-element.8), channel_id=1, replica_groups=mesh['band'=64,'member'=8] {'band'}, use_global_device_ids=true, to_apply=%region_10.11 | all-reduce | flops 512 | bytes 4096 | tf_op jit(solution)/shard_map/psum | solution.py:169
  268.6 0.6 broadcast_multiply_fusion
  269.2 0.9 fusion.7
  270.0 130.9 %all-reduce.3.cloned.1.call-done = (f32[512,512]{1,0:T(8,128)}, f32[512,512]{1,0:T(8,128)}, f32[512,80]{0,1:T(8,128)}) async-done(((f32[512,512]{1,0:T(8,128)}, f32[512,512]{1,0:T(8,128)}, f32[512,80]{0,1:T(8,128)}), (f32[512,512]{1,0:T(8,128)}, f32[512,512]{1,0:T(8,128)}, f32[512,80]{0,1:T(8,128)})) %all-reduce.3.cloned.1.call-update) | async-done | bytes 2261008 | tf_op jit(solution)/shard_map/psum | solution.py:169
  400.9 1.6 multiply_bitcast_fusion.2
  402.5 3.1 multiply_bitcast_fusion
  (14 shorter events, 0.1 us)
Async XLA Ops:
  7.2 40.8 %copy-start = (bf16[512,512]{1,0:T(8,128)(2,1)S(1)}, bf16[512,512]{1,0:T(8,128)(2,1)}, u32[]{:S(2)}) copy-start(bf16[512,512]{1,0:T(8,128)(2,1)} %param.23) | copy-start | bytes 1572868
  10.0 36.3 %all-to-all-start = ((bf16[80,64,8]{0,2,1:T(8,128)(2,1)}), bf16[80,64,8]{0,2,1:T(8,128)(2,1)S(1)}, u32[]{:S(2)}, u32[]{:S(2)}) async-start(bf16[80,64,8]{0,2,1:T(8,128)(2,1)} %bitcast.1), calls=%async_computation | async-start | bytes 262144 | tf_op jit(solution)/shard_map/all_to_all | solution.py:82
  32.1 15.8 %copy-start.4 = (f32[512]{0:T(512)S(1)}, f32[512]{0:T(512)}, u32[]{:S(2)}) copy-start(f32[512]{0:T(512)} %param.22) | copy-start | bytes 6148
  47.9 1.0 copy-start.5
  49.0 0.9 copy-start.2
  49.0 23.5 %copy-start.6 = (f32[80,256]{1,0:T(8,128)S(1)}, f32[80,256]{1,0:T(8,128)}, u32[]{:S(2)}) copy-start(f32[80,256]{1,0:T(8,128)} %param.13) | copy-start | bytes 245764
  51.1 21.4 %all-to-all-start.1 = ((bf16[80,64,8]{0,2,1:T(8,128)(2,1)}), bf16[80,64,8]{0,2,1:T(8,128)(2,1)S(1)}, u32[]{:S(2)}, u32[]{:S(2)}) async-start(bf16[80,64,8]{0,2,1:T(8,128)(2,1)} %bitcast.3), calls=%async_computation.1 | async-start | bytes 262144 | tf_op jit(solution)/shard_map/all_to_all | solution.py:113
  55.7 345.2 %all-reduce.3.cloned.1.call-start = ((), (), s32[]{:S(2)}) async-start(), calls=%async_computation.4 | async-start | bytes 4521984 | tf_op jit(solution)/shard_map/psum | solution.py:169
  72.7 22.3 %copy-start.1 = (f32[80,256]{1,0:T(8,128)}, f32[80,256]{1,0:T(8,128)S(1)}, u32[]{:S(2)}) copy-start(f32[80,256]{1,0:T(8,128)S(1)} %fusion.2) | copy-start | bytes 245764
  95.0 0.8 copy-start.3
Sparse Core Ops, SparseCore 0:
  128.8 272.0 all-reduce.2
where the time goes:
time: 413 us; the launch traced here: 412 us
  blocking collectives  188 us (46%)
  waiting for transfers between devices  162 us (39%)
  starting transfers between devices  23.2 us (6%)
  between operations  14.2 us (3%)
  matrix products  11.4 us (3%)
  other arithmetic  7.49 us (2%)
  local copies, waits for them, and re-layouts  6.88 us (2%)
    psum x1, blocking collectives, body(): lax.psum((up_part, down_part, dec_part, gain_part), 'band')  139 us
    psum x1, waiting for transfers between devices, body(): lax.psum((up_part, down_part, dec_part, gain_part), 'band')  131 us
    all_to_all x1, blocking collectives, body(): lax.all_to_all(slot_grad.reshape(channels, band_count, dec_width), 'band'...  26.3 us
    all_to_all x1, blocking collectives, sent_to_all(): lax.all_to_all(jnp.broadcast_to(array[None], (size, *array.shape)), axis,...  22.2 us
    all_to_all x1, starting transfers between devices, body(): lax.all_to_all(picked.reshape(channels, band_count, enc_width), 'band', s...  18.6 us
    all_to_all x1, waiting for transfers between devices, body(): lax.all_to_all(chosen.reshape(channels, band_count, dec_width), 'band', s...  16.6 us
    all_to_all x1, waiting for transfers between devices, body(): lax.all_to_all(picked.reshape(channels, band_count, enc_width), 'band', s...  14.1 us
  transfers between devices with their start and end apart: 3, of which 3 were waited for; matrix products, arithmetic and copies ran while one was open for 1% of the time, Pallas kernels for 0%

commit v1 on v0

v1 whole, which is shorter than its diff:
```python
import functools
import math

import jax
import jax.numpy as jnp
from jax import lax
from jax.experimental import pallas as pl
from jax.experimental.pallas import tpu as pltpu
from jax.sharding import PartitionSpec as P

MESH = pl.DeviceIdType.MESH
BF = jnp.bfloat16
F32 = jnp.float32
NX = 4
PAD = 128
smooth_sq = 0.01
norm_eps = 1e-05


def dot(a, b, ca=1, cb=0):
    return lax.dot_general(a, b, (((ca,), (cb,)), ((), ())), preferred_element_type=F32)


def slope(diff):
    return diff * lax.rsqrt(diff * diff + smooth_sq)


def pad_rows(a, rows):
    return jnp.concatenate([a, jnp.zeros((rows - a.shape[0], a.shape[1]), a.dtype)], axis=0)


def one_hot(table_ref, width):
    bands, cap = table_ref.shape
    slots = bands * cap
    table = table_ref[...].astype(F32).astype(BF)
    row = lax.broadcasted_iota(jnp.int32, (slots, bands), 0)
    col = lax.broadcasted_iota(jnp.int32, (slots, bands), 1)
    owner = jnp.where(row // cap == col, 1.0, 0.0).astype(BF)
    spread = dot(owner, table)
    row = lax.broadcasted_iota(jnp.int32, (slots, cap), 0)
    col = lax.broadcasted_iota(jnp.int32, (slots, cap), 1)
    spread = jnp.where(row % cap == col, spread, 0.0).astype(BF)
    wide = dot(spread, jnp.ones((cap, width), BF))
    lanes = lax.broadcasted_iota(jnp.int32, (slots, width), 1).astype(F32)
    return jnp.where(wide == lanes, 1.0, 0.0)


def step_kernel(
    field, noise, target, weight, enc_send, enc_recv, dec_send, dec_recv,
    lift, mixing, expand, contract, readout,
    stu_out, grad_out, sums_out,
    send1, recv1, send2, recv2, send3, recv3,
    teach, stu, stus, enc_land, dec_pick, dec_land, fill, readp, liftp, both,
    normed_t, hidden_t, next_t, state, hidden_pre, dsilu, grad_b,
    sums, from_x, part, from_z, full,
    s1, r1, s2, r2, s3, r3, st, rt, ss, rs, sx, rx, sz, rz, sg, rg, sh, rh, l1, l2, l3,
):
    bands = send1.shape[0]
    members = teach.shape[0]
    nz = bands // NX
    b = lax.axis_index("band")
    m = lax.axis_index("member")
    z = b // NX
    x = b % NX
    slots = send1.shape[0] * send1.shape[1]
    channels, cells = field.shape
    nodes = cells

    barrier = pltpu.get_barrier_semaphore()

    def greet_band(k, carry):
        pl.semaphore_signal(
            barrier, inc=1, device_id={"band": (b + k) % bands}, device_id_type=MESH
        )
        return carry

    def greet_member(k, carry):
        pl.semaphore_signal(
            barrier, inc=1, device_id={"member": (m + k) % members}, device_id_type=MESH
        )
        return carry

    lax.fori_loop(1, bands, greet_band, 0)
    lax.fori_loop(1, members, greet_member, 0)

    def to_slots(value, ref):
        ref[...] = value.reshape(ref.shape).astype(BF)

    def from_slots(ref):
        return ref[...].astype(F32).reshape(slots, PAD).astype(BF)

    def band_copy(src, dst, ssem, rsem, peer):
        return pltpu.make_async_remote_copy(
            src_ref=src, dst_ref=dst, send_sem=ssem, recv_sem=rsem,
            device_id={"band": peer}, device_id_type=MESH,
        )

    def exchange(send, recv, ssem, rsem):
        def go(k, carry):
            peer = (b + k) % bands
            band_copy(send.at[peer], recv.at[b], ssem, rsem, peer).start()
            return carry

        lax.fori_loop(1, bands, go, 0)
        recv[pl.ds(b, 1)] = send[pl.ds(b, 1)]

    def whole(send, recv, ssem, rsem):
        some = pl.ds(0, bands - 1)
        return band_copy(send.at[some], recv.at[some], ssem, rsem, (b + 1) % bands)

    def member_copy(src, dst, ssem, rsem, peer):
        return pltpu.make_async_remote_copy(
            src_ref=src, dst_ref=dst, send_sem=ssem, recv_sem=rsem,
            device_id={"member": peer}, device_id_type=MESH,
        )

    inputs = pad_rows((field[...] + noise[...].astype(F32)).astype(BF).astype(F32), PAD).astype(BF)
    to_slots(dot(one_hot(enc_send, cells).astype(BF), inputs, 1, 1), send1)
    pl.semaphore_wait(barrier, bands - 1 + members - 1)
    exchange(send1, recv1, s1, r1)

    def send_target(k, carry):
        member_copy(target, teach.at[m], st, rt, (m + k) % members).start()
        return carry

    lax.fori_loop(1, members, send_target, 0)
    teach[pl.ds(m, 1)] = target[...][None]

    land = one_hot(enc_recv, nodes).T
    enc_land[...] = land.astype(BF)
    edge_scale = 1.0 / jnp.maximum(jnp.sum(land, axis=1, keepdims=True), 1.0)
    liftp[...] = pad_rows(lift[...].astype(F32), PAD).astype(BF)
    readp[...] = jnp.zeros(readp.shape, BF)
    readp[:, :channels] = readout[...]
    both[...] = dot(contract[...], readp[...]).astype(BF)
    pick = one_hot(dec_send, nodes)
    dec_pick[...] = pick.astype(BF)
    dec_land[...] = pick.T.astype(BF)
    cover = one_hot(dec_recv, cells)
    fill[...] = cover.astype(BF)
    inverse = 1.0 / jnp.maximum(jnp.sum(cover, axis=0, keepdims=True), 1.0)

    whole(send1, recv1, s1, r1).wait_recv()
    rows = jax.nn.silu(dot(from_slots(recv1), liftp[...])).astype(BF)
    state[...] = dot(enc_land[...], rows) * edge_scale
    recip = lax.rsqrt(jnp.mean(state[...] * state[...], axis=1, keepdims=True) + norm_eps)
    normed = (state[...] * recip * mixing[...]).astype(BF)
    hidden_pre[...] = dot(normed, expand[...])
    hidden = jax.nn.silu(hidden_pre[...]).astype(BF)
    next_b = (state[...] + dot(hidden, contract[...])).astype(BF)
    projected = dot(next_b, readp[...]).astype(BF)
    to_slots(dot(dec_pick[...], projected), send2)
    exchange(send2, recv2, s2, r2)

    normed_t[...] = normed.astype(F32).T.astype(BF)
    hidden_t[...] = hidden.astype(F32).T.astype(BF)
    next_t[...] = next_b.astype(F32).T.astype(BF)
    sigma = jax.nn.sigmoid(hidden_pre[...])
    dsilu[...] = sigma * (1.0 + hidden_pre[...] * (1.0 - sigma))

    def every_target():
        some = pl.ds(0, members - 1)
        return member_copy(teach.at[some], teach.at[some], st, rt, (m + 1) % members)

    every_target().wait_recv()
    whole(send2, recv2, s2, r2).wait_recv()
    grid_sum = dot(from_slots(recv2), fill[...], 0, 0)[:channels]
    mine = field[...] + grid_sum * inverse
    stu[...] = mine

    def send_student(k, carry):
        member_copy(stu, stus.at[m], ss, rs, (m + k) % members).start()
        return carry

    lax.fori_loop(1, members, send_student, 0)
    stu_copy = pltpu.make_async_copy(stu, stu_out, l1)
    stu_copy.start()
    pull = jnp.zeros((channels, cells), F32)
    for j in range(members):
        pull = pull + slope(mine - teach[j].astype(F32))
    some = pl.ds(0, members - 1)
    every_student = member_copy(stus.at[some], stus.at[some], ss, rs, (m + 1) % members)
    every_student.wait_recv()
    for j in range(1, members):
        pull = pull - slope(mine - stus[pl.ds((m + j) % members, 1)][0])
    scaled = weight[...].astype(F32) * pull * inverse
    to_slots(dot(fill[...], pad_rows(scaled, PAD).astype(BF), 1, 1), send3)
    exchange(send3, recv3, s3, r3)
    whole(send3, recv3, s3, r3).wait_recv()

    node_grad = dot(dec_land[...], from_slots(recv3)).astype(BF)
    pre = (dot(node_grad, both[...], 1, 1) * dsilu[...]).astype(BF)
    wide = pre.shape[1]
    blocks = sums.shape[:3]
    sums[:, :, :, :wide] = dot(normed_t[...], pre).reshape(*blocks, wide).astype(BF)
    sums[:, :, :, wide : wide + PAD] = dot(next_t[...], node_grad).reshape(*blocks, PAD).astype(BF)
    sums[:, :, :, wide + PAD :] = dot(hidden_t[...], node_grad).reshape(*blocks, PAD).astype(BF)

    def send_x(k, carry):
        to = (x + k) % NX
        band_copy(sums.at[to], from_x.at[k - 1], sx, rx, z * NX + to).start()
        return carry

    lax.fori_loop(1, NX, send_x, 0)

    next_grad = dot(node_grad, readp[...], 1, 1)
    gained = dot(pre, expand[...], 1, 1) * mixing[...]
    inner = jnp.mean(gained * state[...], axis=1, keepdims=True)
    grad_b[...] = (
        next_grad + recip * gained - state[...] * (recip * recip * recip) * inner
    ).astype(BF)
    grad_copy = pltpu.make_async_copy(grad_b, grad_out, l2)
    grad_copy.start()

    three = pl.ds(0, NX - 1)
    next_x = z * NX + (x + 1) % NX
    every_x = band_copy(sums.at[three], from_x, sx, rx, next_x)
    every_x.wait_recv()
    total = sums[pl.ds(x, 1)][0].astype(F32)
    for k in range(NX - 1):
        total = total + from_x[k].astype(F32)
    part[...] = total.astype(BF)

    def send_z(k, carry):
        to = (z + k) % nz
        band_copy(part.at[to], from_z.at[z], sz, rz, to * NX + x).start()
        return carry

    lax.fori_loop(1, nz, send_z, 0)
    from_z[pl.ds(z, 1)] = part[pl.ds(z, 1)]
    others = pl.ds(0, nz - 1)
    next_z = ((z + 1) % nz) * NX + x
    every_z = band_copy(part.at[others], from_z.at[others], sz, rz, next_z)
    every_z.wait_recv()
    piece = jnp.sum(from_z[...].astype(F32), axis=0).astype(BF)
    full[pl.ds(x, 1), pl.ds(z, 1)] = piece[None, None]

    def gather_z(k, carry):
        to = (z + k) % nz
        band_copy(full.at[x, z], full.at[x, z], sg, rg, to * NX + x).start()
        return carry

    lax.fori_loop(1, nz, gather_z, 0)
    all_z = band_copy(full.at[x, others], full.at[x, others], sg, rg, next_z)
    all_z.wait_recv()

    def gather_x(k, carry):
        band_copy(full.at[x], full.at[x], sh, rh, z * NX + (x + k) % NX).start()
        return carry

    lax.fori_loop(1, NX, gather_x, 0)
    all_x = band_copy(full.at[three], full.at[three], sh, rh, next_x)
    all_x.wait_recv()
    sums_copy = pltpu.make_async_copy(full, sums_out, l3)
    sums_copy.start()

    whole(send1, recv1, s1, r1).wait_send()
    whole(send2, recv2, s2, r2).wait_send()
    whole(send3, recv3, s3, r3).wait_send()
    every_target().wait_send()
    every_student.wait_send()
    every_x.wait_send()
    every_z.wait_send()
    all_z.wait_send()
    all_x.wait_send()
    stu_copy.wait()
    grad_copy.wait()
    sums_copy.wait()


def finish_kernel(factor, sums, mixing, expand, readout, up_out, down_out, dec_out, gain_out):
    rows = sums.shape[0] * sums.shape[1]
    lat, channels = readout.shape
    wide = expand.shape[1]
    flat = sums[...].astype(F32).reshape(rows, sums.shape[2])
    up = flat[:, :wide] * factor
    up_out[...] = up
    dec_out[...] = flat[:, wide : wide + channels] * factor
    hn = flat[:, wide + PAD : wide + PAD + channels].astype(BF)
    down_out[...] = dot(hn, readout[...], 1, 1) * factor
    terms = up * expand[...].astype(F32)
    high = terms.astype(BF)
    low = (terms - high.astype(F32)).astype(BF)
    ones = jnp.ones((8, wide), BF)
    gain = dot(ones, high, 1, 1) + dot(ones, low, 1, 1)
    gain_out[...] = gain[:1] / mixing[...]


def body(
    field, noise, target, weight, enc_send, enc_recv, dec_send, dec_recv,
    lift, mixing, expand, contract, readout,
):
    bands = lax.axis_size("band")
    members = lax.axis_size("member")
    nz = bands // NX
    channels, cells = field.shape
    nodes = cells
    cap = enc_send.shape[2]
    slots = bands * cap
    lat, hid = expand.shape
    wide = hid + 2 * PAD
    vmem = pl.BlockSpec(memory_space=pltpu.VMEM)
    anywhere = pl.BlockSpec(memory_space=pl.ANY)
    blocks = (NX, nz, lat // bands)
    dma = pltpu.SemaphoreType.DMA
    mixing_row = mixing[None]
    slot_buffer = pltpu.VMEM((bands, cap, PAD), BF)
    student, grad, sums = pl.pallas_call(
        step_kernel,
        out_shape=(
            jax.ShapeDtypeStruct((channels, cells), F32),
            jax.ShapeDtypeStruct((nodes, lat), BF),
            jax.ShapeDtypeStruct((*blocks, wide), BF),
        ),
        in_specs=[vmem] * 13,
        out_specs=(anywhere, anywhere, anywhere),
        scratch_shapes=[slot_buffer] * 6
        + [
            pltpu.VMEM((members, channels, cells), BF),
            pltpu.VMEM((channels, cells), F32),
            pltpu.VMEM((members, channels, cells), F32),
            pltpu.VMEM((nodes, slots), BF),
            pltpu.VMEM((slots, nodes), BF),
            pltpu.VMEM((nodes, slots), BF),
            pltpu.VMEM((slots, cells), BF),
            pltpu.VMEM((lat, PAD), BF),
            pltpu.VMEM((PAD, lat), BF),
            pltpu.VMEM((hid, PAD), BF),
            pltpu.VMEM((lat, nodes), BF),
            pltpu.VMEM((hid, nodes), BF),
            pltpu.VMEM((lat, nodes), BF),
            pltpu.VMEM((nodes, lat), F32),
            pltpu.VMEM((nodes, hid), F32),
            pltpu.VMEM((nodes, hid), F32),
            pltpu.VMEM((nodes, lat), BF),
            pltpu.VMEM((*blocks, wide), BF),
            pltpu.VMEM((NX - 1, *blocks[1:], wide), BF),
            pltpu.VMEM((*blocks[1:], wide), BF),
            pltpu.VMEM((*blocks[1:], wide), BF),
            pltpu.VMEM((*blocks, wide), BF),
        ]
        + [dma(())] * 21,
        compiler_params=pltpu.CompilerParams(
            collective_id=0, has_side_effects=True, vmem_limit_bytes=60 << 20
        ),
        name="step",
    )(
        field, noise[0], target[0], weight, enc_send[0], enc_recv[0], dec_send[0], dec_recv[0],
        lift, mixing_row, expand, contract, readout,
    )
    factor = 1.0 / math.sqrt(bands * nodes)
    up, down, dec, gain = pl.pallas_call(
        functools.partial(finish_kernel, factor),
        out_shape=(
            jax.ShapeDtypeStruct((lat, hid), F32),
            jax.ShapeDtypeStruct((hid, lat), F32),
            jax.ShapeDtypeStruct((lat, channels), F32),
            jax.ShapeDtypeStruct((1, lat), F32),
        ),
        in_specs=[vmem] * 4,
        out_specs=(vmem,) * 4,
        name="finish",
    )(sums.reshape(bands, lat // bands, wide), mixing_row, expand, readout)
    return student[None], grad[None], up[None], down[None], dec[None], gain


def solution(mesh):
    return jax.shard_map(
        body,
        mesh=mesh,
        in_specs=(
            P(None, "band"),
            P("member", None, "band"),
            P("member", None, "band"),
            P(None, "band"),
            P("band", None, None),
            P("band", None, None),
            P("band", None, None),
            P("band", None, None),
            P(),
            P(),
            P(),
            P(),
            P(),
        ),
        out_specs=(
            P("member", None, "band"),
            P("member", "band", None),
            P("member", None, None),
            P("member", None, None),
            P("member", None, None),
            P("member", None),
        ),
        check_vma=False,
    )
```

time: 413 us -> 125 us (0.30)
  the two profiles are of different devices: /device:TPU:8 before, /device:TPU:1 now
where the time goes in v1:
time: 125 us
  Pallas kernels  116 us (93%)
  local copies, waits for them, and re-layouts  8.79 us (7%)
    pallas_call x1, Pallas kernels, body(): pl.pallas_call(step_kernel, out_shape=(jax.ShapeDtypeStruct((channels, ce...  113 us
    unnamed x16, local copies, waits for them, and re-layouts  8.79 us
    pallas_call x1, Pallas kernels, body(): pl.pallas_call(functools.partial(finish_kernel, factor), out_shape=(jax.S...  3.04 us

profile of v1, /device:TPU:1, one launch (start us, length us, event | category | flops | bytes accessed | tf_op | source)
XLA Modules:
  0.0 125.0 jit_solution(4471987024318455424)
XLA Ops:
  0.6 0.0 copy-start.1
  0.6 1.4 %copy.19 = s32[1,64,8]{2,1,0:T(8,128)} copy(s32[1,64,8]{1,2,0:T(8,128)} %param.17) | data formatting | bytes 4096 | tf_op args[4]
  2.1 1.4 %copy.20 = s32[1,64,8]{2,1,0:T(8,128)} copy(s32[1,64,8]{1,2,0:T(8,128)} %param.18) | data formatting | bytes 4096 | tf_op args[5]
  3.4 0.0 copy-start.3
  3.4 1.4 %copy.21 = s32[1,64,8]{2,1,0:T(8,128)} copy(s32[1,64,8]{1,2,0:T(8,128)} %param.19) | data formatting | bytes 4096 | tf_op args[6]
  4.8 0.0 copy-done.3
  4.8 0.7 copy.22
  5.5 0.0 copy-done.1
  5.5 0.8 copy.23.readout
  6.3 112.5 %step.1 = (f32[80,256]{1,0:T(8,128)}, bf16[256,512]{1,0:T(8,128)(2,1)}, bf16[4,16,8,768]{3,2,1,0:T(8,128)(2,1)}) custom-call(f32[80,256]{1,0:T(8,128)} %field.1, bf16[80,256]{1,0:T(8,128)(2,1)} %bitcast.21, bf16[80,256]{1,0:T(8,128)(2,1)} %bitcast.22, bf16[80,256]{1,0:T(8,128)(2,1)} %weight.1, s32[64,8]{1,0:T(8,128)} %bitcast.16, s32[64,8]{1,0:T(8,128)} %bitcast.17, ...), custom_call_target="tpu_custom_call" | custom-call | tf_op jit(solution)/shard_map/step/pallas_call | solution.py:308
  118.8 3.0 %finish.1 = (f32[512,512]{1,0:T(8,128)}, f32[512,512]{1,0:T(8,128)}, f32[512,80]{1,0:T(8,128)}, f32[1,512]{1,0:T(1,128)}) custom-call(bf16[64,8,768]{2,1,0:T(8,128)(2,1)} %bitcast.13, f32[1,512]{1,0:T(1,128)} %bitcast.24, bf16[512,512]{1,0:T(8,128)(2,1)} %expand.3, bf16[512,80]{1,0:T(8,128)(2,1)} %copy.23.readout), custom_call_target="tpu_custom_call" | custom-call | tf_op jit(solution)/shard_map/finish/pallas_call | solution.py:352
  121.9 0.0 copy-start.2
  121.9 0.0 copy-start
  121.9 1.8 %copy.25 = f32[1,512,80]{1,2,0:T(8,128)} copy(f32[1,512,80]{2,1,0:T(8,128)} %bitcast.15) | data formatting | bytes 327680
  123.7 0.0 copy-done.2
  123.7 0.6 copy.28
  124.3 0.0 copy-done
  124.3 0.7 copy.29
Async XLA Ops:
  0.6 4.9 %copy-start.1 = (bf16[512,80]{0,1:T(8,128)(2,1)S(1)}, bf16[512,80]{0,1:T(8,128)(2,1)}, u32[]{:S(2)}) copy-start(bf16[512,80]{0,1:T(8,128)(2,1)} %param.25) | copy-start | bytes 245764
  3.4 1.4 %copy-start.3 = (s32[1,64,8]{1,2,0:T(8,128)S(1)}, s32[1,64,8]{1,2,0:T(8,128)}, u32[]{:S(2)}) copy-start(s32[1,64,8]{1,2,0:T(8,128)} %param.20) | copy-start | bytes 6148
  121.9 1.8 %copy-start.2 = (f32[80,256]{1,0:T(8,128)S(1)}, f32[80,256]{1,0:T(8,128)}, u32[]{:S(2)}) copy-start(f32[80,256]{1,0:T(8,128)} %get-tuple-element.13) | copy-start | bytes 245764
  121.9 2.4 %copy-start = (bf16[256,512]{1,0:T(8,128)(2,1)S(1)}, bf16[256,512]{1,0:T(8,128)(2,1)}, u32[]{:S(2)}) copy-start(bf16[256,512]{1,0:T(8,128)(2,1)} %get-tuple-element.14) | copy-start | bytes 786436

commit v2 on v1

v2 whole, which is shorter than its diff:
```python
import functools
import math

import jax
import jax.numpy as jnp
from jax import lax
from jax.experimental import pallas as pl
from jax.experimental.pallas import tpu as pltpu
from jax.sharding import PartitionSpec as P

MESH = pl.DeviceIdType.MESH
BF = jnp.bfloat16
F32 = jnp.float32
NX = 4
PAD = 128
smooth_sq = 0.01
norm_eps = 1e-05


def dot(a, b, ca=1, cb=0):
    return lax.dot_general(a, b, (((ca,), (cb,)), ((), ())), preferred_element_type=F32)


def slope(diff):
    return diff * lax.rsqrt(diff * diff + smooth_sq)


def pad_rows(a, rows):
    return jnp.concatenate([a, jnp.zeros((rows - a.shape[0], a.shape[1]), a.dtype)], axis=0)


def one_hot(table_ref, width):
    cap, bands = table_ref.shape
    slots = bands * cap
    table = table_ref[...].astype(F32).astype(BF)
    row = lax.broadcasted_iota(jnp.int32, (slots, bands), 0)
    col = lax.broadcasted_iota(jnp.int32, (slots, bands), 1)
    owner = jnp.where(row // cap == col, 1.0, 0.0).astype(BF)
    spread = dot(owner, table, 1, 1)
    row = lax.broadcasted_iota(jnp.int32, (slots, cap), 0)
    col = lax.broadcasted_iota(jnp.int32, (slots, cap), 1)
    spread = jnp.where(row % cap == col, spread, 0.0).astype(BF)
    wide = dot(spread, jnp.ones((cap, width), BF))
    lanes = lax.broadcasted_iota(jnp.int32, (slots, width), 1).astype(F32)
    return jnp.where(wide == lanes, 1.0, 0.0)


def far_first(j, half):
    return half + (1 - 2 * (j % 2)) * ((j + 1) // 2)


def step_kernel(
    enc_send_in, field_in, noise_in, lift_in, enc_recv_in, dec_send_in, dec_recv_in,
    mixing_in, expand_in, contract_in, readout_in, target_in, weight_in,
    stu_out, grad_out, sums_out,
    enc_send, field, noise, lift, enc_recv, dec_send, dec_recv,
    mixing, expand, contract, readout, target, weight,
    send1, recv1, send2, recv2, send3, recv3,
    teach, stu, stus, enc_land, dec_pick, dec_land, fill, readp, both,
    normed_t, hidden_t, next_t, state, hidden_pre, dsilu, grad_b,
    sums, relay, ahead, from_x, part, from_z, full,
    loads, s1, r1, s2, r2, s3, r3, st, rt, ss, rs, sf, rf,
    s_rel, r_rel, s_x, s_x2, r_x, s_z, r_z, s_gz, r_gz, s_gx, r_gx, s_fw, r_fw, l1, l2, l3,
):
    bands = send1.shape[0]
    members = teach.shape[0]
    nz = bands // NX
    half = nz // 2
    chunks = sums.shape[0]
    b = lax.axis_index("band")
    m = lax.axis_index("member")
    z = b // NX
    x = b % NX
    y = m // 2
    core = m % 2
    slots = send1.shape[0] * send1.shape[1]
    channels, cells = field.shape
    nodes = cells

    into = (
        enc_send, field, noise, lift, enc_recv, dec_send, dec_recv,
        mixing, expand, contract, readout, target, weight,
    )
    out_of = (
        enc_send_in, field_in, noise_in, lift_in, enc_recv_in, dec_send_in, dec_recv_in,
        mixing_in, expand_in, contract_in, readout_in, target_in, weight_in,
    )
    load = [pltpu.make_async_copy(o, i, loads.at[k]) for k, (o, i) in enumerate(zip(out_of, into))]
    for copy in load[:3]:
        copy.start()

    def peer_of(t):
        return ((z + far_first(t // NX, half)) % nz) * NX + (x + NX - 1 - t % NX) % NX

    barrier = pltpu.get_barrier_semaphore()

    def greet_band(t, carry):
        pl.semaphore_signal(barrier, inc=1, device_id={"band": peer_of(t)}, device_id_type=MESH)
        return carry

    def greet_member(k, carry):
        pl.semaphore_signal(
            barrier, inc=1, device_id={"member": (m + k) % members}, device_id_type=MESH
        )
        return carry

    lax.fori_loop(0, bands - 1, greet_band, 0)
    lax.fori_loop(1, members, greet_member, 0)
    for copy in load[3:]:
        copy.start()

    def to_slots(value, ref):
        ref[...] = value.reshape(ref.shape).astype(BF)

    def from_slots(ref):
        return ref[...].astype(F32).reshape(slots, PAD).astype(BF)

    def band_copy(src, dst, ssem, rsem, peer):
        return pltpu.make_async_remote_copy(
            src_ref=src, dst_ref=dst, send_sem=ssem, recv_sem=rsem,
            device_id={"band": peer}, device_id_type=MESH,
        )

    def member_copy(src, dst, ssem, rsem, peer):
        return pltpu.make_async_remote_copy(
            src_ref=src, dst_ref=dst, send_sem=ssem, recv_sem=rsem,
            device_id={"member": peer}, device_id_type=MESH,
        )

    def exchange(send, recv, ssem, rsem):
        def go(t, carry):
            peer = peer_of(t)
            band_copy(send.at[peer], recv.at[b], ssem, rsem, peer).start()
            return carry

        lax.fori_loop(0, bands - 1, go, 0)
        recv[pl.ds(b, 1)] = send[pl.ds(b, 1)]

    def whole(send, recv, ssem, rsem):
        some = pl.ds(0, bands - 1)
        return band_copy(send.at[some], recv.at[some], ssem, rsem, (b + 1) % bands)

    for copy in load[:3]:
        copy.wait()
    inputs = pad_rows((field[...] + noise[...].astype(F32)).astype(BF).astype(F32), PAD).astype(BF)
    to_slots(dot(one_hot(enc_send, cells).astype(BF), inputs, 1, 1), send1)
    pl.semaphore_wait(barrier, bands - 1 + members - 1)
    exchange(send1, recv1, s1, r1)
    for copy in load[3:]:
        copy.wait()

    def send_target(k, carry):
        member_copy(target, teach.at[m], st, rt, (m + k) % members).start()
        return carry

    lax.fori_loop(1, members, send_target, 0)
    teach[pl.ds(m, 1)] = target[...][None]

    land = one_hot(enc_recv, nodes).T
    enc_land[...] = land.astype(BF)
    edge_scale = 1.0 / jnp.maximum(jnp.sum(land, axis=1, keepdims=True), 1.0)
    lift_rows = pad_rows(lift[...].astype(F32), PAD).astype(BF)
    readp[...] = pad_rows(readout[...].astype(F32), PAD).astype(BF)
    both[...] = dot(contract[...], readp[...], 1, 1).astype(BF)
    pick = one_hot(dec_send, nodes)
    dec_pick[...] = pick.astype(BF)
    dec_land[...] = pick.T.astype(BF)
    cover = one_hot(dec_recv, cells)
    fill[...] = cover.astype(BF)
    inverse = 1.0 / jnp.maximum(jnp.sum(cover, axis=0, keepdims=True), 1.0)

    whole(send1, recv1, s1, r1).wait_recv()
    rows = jax.nn.silu(dot(from_slots(recv1), lift_rows)).astype(BF)
    state[...] = dot(enc_land[...], rows) * edge_scale
    recip = lax.rsqrt(jnp.mean(state[...] * state[...], axis=1, keepdims=True) + norm_eps)
    normed = (state[...] * recip * mixing[...]).astype(BF)
    hidden_pre[...] = dot(normed, expand[...])
    hidden = jax.nn.silu(hidden_pre[...]).astype(BF)
    next_b = (state[...] + dot(hidden, contract[...])).astype(BF)
    projected = dot(next_b, readp[...], 1, 1).astype(BF)
    to_slots(dot(dec_pick[...], projected), send2)
    exchange(send2, recv2, s2, r2)

    normed_t[...] = normed.astype(F32).T.astype(BF)
    hidden_t[...] = hidden.astype(F32).T.astype(BF)
    next_t[...] = next_b.astype(F32).T.astype(BF)
    sigma = jax.nn.sigmoid(hidden_pre[...])
    dsilu[...] = sigma * (1.0 + hidden_pre[...] * (1.0 - sigma))

    seven = pl.ds(0, members - 1)
    every_target = member_copy(teach.at[seven], teach.at[seven], st, rt, (m + 1) % members)
    every_target.wait_recv()
    whole(send2, recv2, s2, r2).wait_recv()
    grid_sum = dot(from_slots(recv2), fill[...], 0, 0)[:channels]
    mine = field[...] + grid_sum * inverse
    stu[...] = mine

    chips = members // 2
    partner = y * 2 + 1 - core

    def chip(k):
        return ((y + k) % chips) * 2

    direct = [
        member_copy(stu, stus.at[m], ss.at[k], rs.at[k], chip(k) + core if k else partner)
        for k in range(chips)
    ]
    for k in (2, 1, 3, 0):
        direct[k].start()
    stu_copy = pltpu.make_async_copy(stu, stu_out, l1)
    stu_copy.start()
    pull = jnp.zeros((channels, cells), F32)
    for j in range(members):
        pull = pull + slope(mine - teach[j].astype(F32))
    passed = []
    for k in (0, 1, 3, 2):
        direct[k].wait_recv()
        if k:
            source = chip(chips - k) + core
            copy = member_copy(stus.at[source], stus.at[source], sf.at[k], rf.at[k], partner)
            copy.start()
            passed.append((k, copy))
        else:
            source = partner
        pull = pull - slope(mine - stus[pl.ds(source, 1)][0])
    for k, copy in passed:
        copy.wait_recv()
        pull = pull - slope(mine - stus[pl.ds(chip(chips - k) + 1 - core, 1)][0])
    scaled = weight[...].astype(F32) * pull * inverse
    to_slots(dot(fill[...], pad_rows(scaled, PAD).astype(BF), 1, 1), send3)
    exchange(send3, recv3, s3, r3)
    whole(send3, recv3, s3, r3).wait_recv()

    node_grad = dot(dec_land[...], from_slots(recv3)).astype(BF)
    up_x = z * NX + (x + 1) % NX
    down_x = z * NX + (x + NX - 1) % NX
    right = (x + 1) % NX
    left = (x + NX - 1) % NX
    across = (x + 2) % NX
    low = pl.ds(0, half)
    high = pl.ds(half, half)
    quarter = sums.shape[1:4]
    wide = sums.shape[4]

    def launch(c):
        g = sums.at[c]
        band_copy(g.at[across, low], relay.at[c, 0], s_rel.at[c], r_rel.at[c], up_x).start()
        band_copy(g.at[across, high], relay.at[c, 1], s_rel.at[c], r_rel.at[c], down_x).start()
        band_copy(g.at[right, high], from_x.at[c, 0, high], s_x.at[c], r_x.at[c], up_x).start()
        band_copy(g.at[left, low], from_x.at[c, 1, low], s_x.at[c], r_x.at[c], down_x).start()

    last = chunks - 1
    sums[last, :, :, :, :PAD] = dot(next_t[...], node_grad).reshape(*quarter, PAD).astype(BF)
    sums[last, :, :, :, PAD:] = dot(hidden_t[...], node_grad).reshape(*quarter, PAD).astype(BF)
    launch(last)
    pre = (dot(node_grad, both[...], 1, 1) * dsilu[...]).astype(BF)
    for c in range(last):
        some = pre[:, c * wide : (c + 1) * wide]
        sums[c] = dot(normed_t[...], some).reshape(*quarter, wide).astype(BF)
        launch(c)

    order = [last, *range(last)]
    every_rel = [
        band_copy(relay.at[c], relay.at[c], s_rel.at[c], r_rel.at[c], up_x) for c in range(chunks)
    ]
    for c in order:
        every_rel[c].wait_recv()
        mine_up = sums[c, pl.ds(right, 1), low][0].astype(F32) + relay[c, 0].astype(F32)
        mine_down = sums[c, pl.ds(left, 1), high][0].astype(F32) + relay[c, 1].astype(F32)
        ahead[c, 0] = mine_up.astype(BF)
        ahead[c, 1] = mine_down.astype(BF)
        band_copy(ahead.at[c, 0], from_x.at[c, 0, low], s_x2.at[c], r_x.at[c], up_x).start()
        band_copy(ahead.at[c, 1], from_x.at[c, 1, high], s_x2.at[c], r_x.at[c], down_x).start()

    ring = pl.ds(0, nz - 1)
    next_z = ((z + 1) % nz) * NX + x
    for c in order:
        band_copy(from_x.at[c], from_x.at[c], s_x.at[c], r_x.at[c], up_x).wait_recv()
        total = sums[c, pl.ds(x, 1)][0].astype(F32)
        total = total + from_x[c, 0].astype(F32) + from_x[c, 1].astype(F32)
        part[c] = total.astype(BF)

        def send_z(j, carry, c=c):
            to = (z + far_first(j, half)) % nz
            band_copy(
                part.at[c, to], from_z.at[c, z], s_z.at[c], r_z.at[c], to * NX + x
            ).start()
            return carry

        lax.fori_loop(0, nz - 1, send_z, 0)
        from_z[c, pl.ds(z, 1)] = part[c, pl.ds(z, 1)]

    next_grad = dot(node_grad, readp[...])
    gained = dot(pre, expand[...], 1, 1) * mixing[...]
    inner = jnp.mean(gained * state[...], axis=1, keepdims=True)
    grad_b[...] = (
        next_grad + recip * gained - state[...] * (recip * recip * recip) * inner
    ).astype(BF)
    grad_copy = pltpu.make_async_copy(grad_b, grad_out, l2)
    grad_copy.start()

    every_z = [
        band_copy(from_z.at[c, ring], from_z.at[c, ring], s_z.at[c], r_z.at[c], next_z)
        for c in range(chunks)
    ]
    all_z = [
        band_copy(full.at[c, x, ring], full.at[c, x, ring], s_gz.at[c], r_gz.at[c], next_z)
        for c in range(chunks)
    ]
    for c in order:
        every_z[c].wait_recv()
        piece = jnp.sum(from_z[c].astype(F32), axis=0).astype(BF)
        full[c, pl.ds(x, 1), pl.ds(z, 1)] = piece[None, None]

        def gather_z(j, carry, c=c):
            to = (z + far_first(j, half)) % nz
            mine_z = full.at[c, x, z]
            band_copy(mine_z, mine_z, s_gz.at[c], r_gz.at[c], to * NX + x).start()
            return carry

        lax.fori_loop(0, nz - 1, gather_z, 0)

    gx = []
    for c in order:
        all_z[c].wait_recv()
        mine_x = full.at[c, x]
        pair = (
            band_copy(mine_x, mine_x, s_gx.at[c, 0], r_gx.at[c, 0], up_x),
            band_copy(mine_x, mine_x, s_gx.at[c, 1], r_gx.at[c, 1], down_x),
        )
        for copy in pair:
            copy.start()
        gx.append(pair)
    fw = []
    for c, pair in zip(order, gx):
        pair[0].wait_recv()
        there = full.at[c, left, low]
        band_copy(there, there, s_fw.at[c], r_fw.at[c], up_x).start()
        pair[1].wait_recv()
        there = full.at[c, right, high]
        band_copy(there, there, s_fw.at[c], r_fw.at[c], down_x).start()
        fw.append(band_copy(full.at[c, across], full.at[c, across], s_fw.at[c], r_fw.at[c], up_x))
    sums_copies = []
    for c, copy in zip(order, fw):
        copy.wait_recv()
        sums_copies.append(pltpu.make_async_copy(full.at[c], sums_out.at[c], l3.at[c]))
        sums_copies[-1].start()

    whole(send1, recv1, s1, r1).wait_send()
    whole(send2, recv2, s2, r2).wait_send()
    whole(send3, recv3, s3, r3).wait_send()
    every_target.wait_send()
    for copy in direct:
        copy.wait_send()
    for k, copy in passed:
        copy.wait_send()
    for i, c in enumerate(order):
        every_rel[c].wait_send()
        band_copy(sums.at[c, 0], sums.at[c, 0], s_x.at[c], r_x.at[c], up_x).wait_send()
        band_copy(ahead.at[c], ahead.at[c], s_x2.at[c], r_x.at[c], up_x).wait_send()
        every_z[c].wait_send()
        all_z[c].wait_send()
        for copy in gx[i]:
            copy.wait_send()
        fw[i].wait_send()
    stu_copy.wait()
    grad_copy.wait()
    for copy in sums_copies:
        copy.wait()


def finish_kernel(
    factor, sums, mixing, expand, readout, stu_in, grad_in,
    up_out, down_out, dec_out, gain_out, stu_out, grad_out,
    up, down, dec, stu, grad, sems,
):
    chunks, pieces, depth, wide = sums.shape
    rows = pieces * depth
    lat = expand.shape[1]
    channels = readout.shape[0]
    ins = [
        pltpu.make_async_copy(stu_in, stu, sems.at[0]),
        pltpu.make_async_copy(grad_in, grad, sems.at[1]),
    ]
    for copy in ins:
        copy.start()
    low = sums[chunks - 1].astype(F32).reshape(rows, wide)
    outs = []

    def send(src, dst):
        outs.append(pltpu.make_async_copy(src, dst, sems.at[2 + len(outs)]))
        outs[-1].start()

    for c in range(chunks - 1):
        up[:, c * wide : (c + 1) * wide] = sums[c].astype(F32).reshape(rows, wide) * factor
    send(up, up_out)
    read_rows = pad_rows(readout[...].astype(F32), PAD).astype(BF)
    down[...] = dot(low[:, PAD:].astype(BF), read_rows) * factor
    send(down, down_out)
    dec[...] = low[:, :PAD].T[:channels] * factor
    send(dec, dec_out)
    for copy in ins:
        copy.wait()
    send(stu, stu_out)
    send(grad, grad_out)
    terms = up[...] * expand[...].astype(F32)
    high = terms.astype(BF)
    rest = (terms - high.astype(F32)).astype(BF)
    ones = jnp.ones((8, lat), BF)
    gain = dot(ones, high, 1, 1) + dot(ones, rest, 1, 1)
    gain_out[...] = gain[:1] / mixing[...]
    for copy in outs:
        copy.wait()


CHUNK = 256


def body(
    field, noise, target, weight, enc_send, enc_recv, dec_send, dec_recv,
    lift, mixing, expand, contract, readout,
):
    bands = lax.axis_size("band")
    members = lax.axis_size("member")
    nz = bands // NX
    channels, cells = field.shape
    nodes = cells
    cap = enc_send.shape[2]
    slots = bands * cap
    lat, hid = expand.shape
    chunks = (hid + 2 * PAD) // CHUNK
    vmem = pl.BlockSpec(memory_space=pltpu.VMEM)
    anywhere = pl.BlockSpec(memory_space=pl.ANY)
    quarter = (nz, lat // bands, CHUNK)
    half = (nz // 2, lat // bands, CHUNK)
    dma = pltpu.SemaphoreType.DMA
    mixing_row = mixing[None]
    read_t = readout.T
    slot_buffer = pltpu.VMEM((bands, cap, PAD), BF)
    ins = (
        enc_send[0].T, field, noise[0], lift, enc_recv[0].T, dec_send[0].T, dec_recv[0].T,
        mixing_row, expand, contract, read_t, target[0], weight,
    )
    student, grad, sums = pl.pallas_call(
        step_kernel,
        out_shape=(
            jax.ShapeDtypeStruct((channels, cells), F32),
            jax.ShapeDtypeStruct((nodes, lat), BF),
            jax.ShapeDtypeStruct((chunks, NX, *quarter), BF),
        ),
        in_specs=[anywhere] * len(ins),
        out_specs=(anywhere, anywhere, anywhere),
        scratch_shapes=[pltpu.VMEM(a.shape, a.dtype) for a in ins]
        + [slot_buffer] * 6
        + [
            pltpu.VMEM((members, channels, cells), BF),
            pltpu.VMEM((channels, cells), F32),
            pltpu.VMEM((members, channels, cells), F32),
            pltpu.VMEM((nodes, slots), BF),
            pltpu.VMEM((slots, nodes), BF),
            pltpu.VMEM((nodes, slots), BF),
            pltpu.VMEM((slots, cells), BF),
            pltpu.VMEM((PAD, lat), BF),
            pltpu.VMEM((hid, PAD), BF),
            pltpu.VMEM((lat, nodes), BF),
            pltpu.VMEM((hid, nodes), BF),
            pltpu.VMEM((lat, nodes), BF),
            pltpu.VMEM((nodes, lat), F32),
            pltpu.VMEM((nodes, hid), F32),
            pltpu.VMEM((nodes, hid), F32),
            pltpu.VMEM((nodes, lat), BF),
            pltpu.VMEM((chunks, NX, *quarter), BF),
            pltpu.VMEM((chunks, 2, *half), BF),
            pltpu.VMEM((chunks, 2, *half), BF),
            pltpu.VMEM((chunks, 2, *quarter), BF),
            pltpu.VMEM((chunks, *quarter), BF),
            pltpu.VMEM((chunks, *quarter), BF),
            pltpu.VMEM((chunks, NX, *quarter), BF),
        ]
        + [dma((len(ins),))]
        + [dma(())] * 8
        + [dma((members // 2,))] * 4
        + [dma((chunks,))] * 9
        + [dma((chunks, 2))] * 2
        + [dma((chunks,))] * 2
        + [dma(()), dma(()), dma((chunks,))],
        compiler_params=pltpu.CompilerParams(
            collective_id=0, has_side_effects=True, vmem_limit_bytes=60 << 20
        ),
        name="step",
    )(*ins)
    factor = 1.0 / math.sqrt(bands * nodes)
    outs = (
        jax.ShapeDtypeStruct((lat, hid), F32),
        jax.ShapeDtypeStruct((hid, lat), F32),
        jax.ShapeDtypeStruct((channels, lat), F32),
        jax.ShapeDtypeStruct((1, lat), F32),
        jax.ShapeDtypeStruct((channels, cells), F32),
        jax.ShapeDtypeStruct((nodes, lat), BF),
    )
    up, down, dec, gain, student, grad = pl.pallas_call(
        functools.partial(finish_kernel, factor),
        out_shape=outs,
        in_specs=[vmem] * 4 + [anywhere] * 2,
        out_specs=(anywhere, anywhere, anywhere, vmem, anywhere, anywhere),
        scratch_shapes=[pltpu.VMEM(outs[i].shape, outs[i].dtype) for i in (0, 1, 2, 4, 5)]
        + [dma((7,))],
        name="finish",
    )(sums.reshape(chunks, bands, lat // bands, CHUNK), mixing_row, expand, read_t, student, grad)
    return student[None], grad[None], up[None], down[None], dec.T[None], gain


def solution(mesh):
    return jax.shard_map(
        body,
        mesh=mesh,
        in_specs=(
            P(None, "band"),
            P("member", None, "band"),
            P("member", None, "band"),
            P(None, "band"),
            P("band", None, None),
            P("band", None, None),
            P("band", None, None),
            P("band", None, None),
            P(),
            P(),
            P(),
            P(),
            P(),
        ),
        out_specs=(
            P("member", None, "band"),
            P("member", "band", None),
            P("member", None, None),
            P("member", None, None),
            P("member", None, None),
            P("member", None),
        ),
        check_vma=False,
    )
```

time: 125 us -> 95 us (0.76)
  the two profiles are of different devices: /device:TPU:1 before, /device:TPU:4 now
where the time goes in v2:
time: 95 us; the launch traced here: 94.9 us
  Pallas kernels  94.2 us (99%)
    pallas_call x1, Pallas kernels, body(): pl.pallas_call(step_kernel, out_shape=(jax.ShapeDtypeStruct((channels, ce...  90.5 us
    pallas_call x1, Pallas kernels, body(): pl.pallas_call(functools.partial(finish_kernel, factor), out_shape=outs,...  3.75 us

profile of v2, /device:TPU:4, one launch (start us, length us, event | category | flops | bytes accessed | tf_op | source)
XLA Modules:
  0.0 94.9 jit_solution(7588501411517824693)
XLA Ops:
  0.6 90.5 %step.1 = (f32[80,256]{1,0:T(8,128)}, bf16[256,512]{1,0:T(8,128)(2,1)}, bf16[3,4,16,8,256]{4,3,2,1,0:T(8,128)(2,1)}) custom-call(s32[8,64]{1,0:T(8,128)} %bitcast.31, f32[80,256]{1,0:T(8,128)} %field_in.1, bf16[80,256]{1,0:T(8,128)(2,1)} %bitcast.27, bf16[80,512]{1,0:T(8,128)(2,1)} %lift_in.1, s32[8,64]{1,0:T(8,128)} %bitcast.32, s32[8,64]{1,0:T(8,128)} %bitcast.33, ...), custom_call_target="tpu_custom_call" | custom-call | tf_op jit(solution)/shard_map/step/pallas_call | solution.py:444
  91.1 3.8 %finish.1 = (f32[512,512]{1,0:T(8,128)}, f32[512,512]{1,0:T(8,128)}, f32[80,512]{1,0:T(8,128)}, f32[1,512]{1,0:T(1,128)}, f32[80,256]{1,0:T(8,128)}, /*index=5*/bf16[256,512]{1,0:T(8,128)(2,1)}) custom-call(bf16[3,64,8,256]{3,2,1,0:T(8,128)(2,1)} %bitcast.24, f32[1,512]{1,0:T(1,128)} %bitcast.30, bf16[512,512]{1,0:T(8,128)(2,1)} %expand.1, ...), custom_call_target="tpu_custom_call" | custom-call | tf_op jit(solution)/shard_map/finish/pallas_call | solution.py:501

commit v3 on v2

--- a/solution.py
+++ b/solution.py
@@ -50,17 +50,17 @@
 
 
 def step_kernel(
-    enc_send_in, field_in, noise_in, lift_in, enc_recv_in, dec_send_in, dec_recv_in,
+    factor, enc_send_in, field_in, noise_in, lift_in, enc_recv_in, dec_send_in, dec_recv_in,
     mixing_in, expand_in, contract_in, readout_in, target_in, weight_in,
-    stu_out, grad_out, sums_out,
+    stu, grad_b, up_out, down_out, dec_out, gain_out,
     enc_send, field, noise, lift, enc_recv, dec_send, dec_recv,
     mixing, expand, contract, readout, target, weight,
     send1, recv1, send2, recv2, send3, recv3,
-    teach, stu, stus, enc_land, dec_pick, dec_land, fill, readp, both,
-    normed_t, hidden_t, next_t, state, hidden_pre, dsilu, grad_b,
-    sums, relay, ahead, from_x, part, from_z, full,
+    teach, stus, enc_land, dec_pick, dec_land, fill, readp, both,
+    normed_t, hidden_t, next_t, state, hidden_pre, dsilu,
+    sums, from_x, part, from_z, full,
     loads, s1, r1, s2, r2, s3, r3, st, rt, ss, rs, sf, rf,
-    s_rel, r_rel, s_x, s_x2, r_x, s_z, r_z, s_gz, r_gz, s_gx, r_gx, s_fw, r_fw, l1, l2, l3,
+    s_x, r_x, s_z, r_z, s_gz, r_gz, s_gx, r_gx,
 ):
     bands = send1.shape[0]
     members = teach.shape[0]
@@ -207,8 +207,6 @@
     ]
     for k in (2, 1, 3, 0):
         direct[k].start()
-    stu_copy = pltpu.make_async_copy(stu, stu_out, l1)
-    stu_copy.start()
     pull = jnp.zeros((channels, cells), F32)
     for j in range(members):
         pull = pull + slope(mine - teach[j].astype(F32))
@@ -232,22 +230,18 @@
     whole(send3, recv3, s3, r3).wait_recv()
 
     node_grad = dot(dec_land[...], from_slots(recv3)).astype(BF)
-    up_x = z * NX + (x + 1) % NX
-    down_x = z * NX + (x + NX - 1) % NX
-    right = (x + 1) % NX
-    left = (x + NX - 1) % NX
-    across = (x + 2) % NX
-    low = pl.ds(0, half)
-    high = pl.ds(half, half)
     quarter = sums.shape[1:4]
     wide = sums.shape[4]
+    three = pl.ds(0, NX - 1)
+    next_x = z * NX + (x + 1) % NX
+    far_x = (2, 1, 3)
 
     def launch(c):
-        g = sums.at[c]
-        band_copy(g.at[across, low], relay.at[c, 0], s_rel.at[c], r_rel.at[c], up_x).start()
-        band_copy(g.at[across, high], relay.at[c, 1], s_rel.at[c], r_rel.at[c], down_x).start()
-        band_copy(g.at[right, high], from_x.at[c, 0, high], s_x.at[c], r_x.at[c], up_x).start()
-        band_copy(g.at[left, low], from_x.at[c, 1, low], s_x.at[c], r_x.at[c], down_x).start()
+        for k in far_x:
+            to = (x + k) % NX
+            band_copy(
+                sums.at[c, to], from_x.at[c, k - 1], s_x.at[c], r_x.at[c], z * NX + to
+            ).start()
 
     last = chunks - 1
     sums[last, :, :, :, :PAD] = dot(next_t[...], node_grad).reshape(*quarter, PAD).astype(BF)
@@ -260,24 +254,17 @@
         launch(c)
 
     order = [last, *range(last)]
-    every_rel = [
-        band_copy(relay.at[c], relay.at[c], s_rel.at[c], r_rel.at[c], up_x) for c in range(chunks)
+    every_x = [
+        band_copy(sums.at[c, three], from_x.at[c], s_x.at[c], r_x.at[c], next_x)
+        for c in range(chunks)
     ]
-    for c in order:
-        every_rel[c].wait_recv()
-        mine_up = sums[c, pl.ds(right, 1), low][0].astype(F32) + relay[c, 0].astype(F32)
-        mine_down = sums[c, pl.ds(left, 1), high][0].astype(F32) + relay[c, 1].astype(F32)
-        ahead[c, 0] = mine_up.astype(BF)
-        ahead[c, 1] = mine_down.astype(BF)
-        band_copy(ahead.at[c, 0], from_x.at[c, 0, low], s_x2.at[c], r_x.at[c], up_x).start()
-        band_copy(ahead.at[c, 1], from_x.at[c, 1, high], s_x2.at[c], r_x.at[c], down_x).start()
-
     ring = pl.ds(0, nz - 1)
     next_z = ((z + 1) % nz) * NX + x
     for c in order:
-        band_copy(from_x.at[c], from_x.at[c], s_x.at[c], r_x.at[c], up_x).wait_recv()
+        every_x[c].wait_recv()
         total = sums[c, pl.ds(x, 1)][0].astype(F32)
-        total = total + from_x[c, 0].astype(F32) + from_x[c, 1].astype(F32)
+        for k in range(NX - 1):
+            total = total + from_x[c, k].astype(F32)
         part[c] = total.astype(BF)
 
         def send_z(j, carry, c=c):
@@ -296,8 +283,6 @@
     grad_b[...] = (
         next_grad + recip * gained - state[...] * (recip * recip * recip) * inner
     ).astype(BF)
-    grad_copy = pltpu.make_async_copy(grad_b, grad_out, l2)
-    grad_copy.start()
 
     every_z = [
         band_copy(from_z.at[c, ring], from_z.at[c, ring], s_z.at[c], r_z.at[c], next_z)
@@ -320,31 +305,34 @@
 
         lax.fori_loop(0, nz - 1, gather_z, 0)
 
-    gx = []
+    all_x = [
+        band_copy(full.at[c, three], full.at[c, three], s_gx.at[c], r_gx.at[c], next_x)
+        for c in range(chunks)
+    ]
     for c in order:
         all_z[c].wait_recv()
-        mine_x = full.at[c, x]
-        pair = (
-            band_copy(mine_x, mine_x, s_gx.at[c, 0], r_gx.at[c, 0], up_x),
-            band_copy(mine_x, mine_x, s_gx.at[c, 1], r_gx.at[c, 1], down_x),
-        )
-        for copy in pair:
-            copy.start()
-        gx.append(pair)
-    fw = []
-    for c, pair in zip(order, gx):
-        pair[0].wait_recv()
-        there = full.at[c, left, low]
-        band_copy(there, there, s_fw.at[c], r_fw.at[c], up_x).start()
-        pair[1].wait_recv()
-        there = full.at[c, right, high]
-        band_copy(there, there, s_fw.at[c], r_fw.at[c], down_x).start()
-        fw.append(band_copy(full.at[c, across], full.at[c, across], s_fw.at[c], r_fw.at[c], up_x))
-    sums_copies = []
-    for c, copy in zip(order, fw):
-        copy.wait_recv()
-        sums_copies.append(pltpu.make_async_copy(full.at[c], sums_out.at[c], l3.at[c]))
-        sums_copies[-1].start()
+        for k in far_x:
+            mine_x = full.at[c, x]
+            band_copy(mine_x, mine_x, s_gx.at[c], r_gx.at[c], z * NX + (x + k) % NX).start()
+
+    rows = quarter[0] * quarter[1] * quarter[2]
+    ones = jnp.ones((8, wide), BF)
+    gain = jnp.zeros((8, rows), F32)
+    for c in order:
+        all_x[c].wait_recv()
+        some = full[c].astype(F32).reshape(rows, wide)
+        if c == last:
+            down_out[...] = dot(some[:, PAD:].astype(BF), readp[...]) * factor
+            dec_out[...] = some[:, :PAD].T[:channels] * factor
+        else:
+            at = slice(c * wide, (c + 1) * wide)
+            some = some * factor
+            up_out[:, at] = some
+            terms = some * expand[:, at].astype(F32)
+            main = terms.astype(BF)
+            rest = (terms - main.astype(F32)).astype(BF)
+            gain = gain + dot(ones, main, 1, 1) + dot(ones, rest, 1, 1)
+    gain_out[...] = gain[:1] / mixing[...]
 
     whole(send1, recv1, s1, r1).wait_send()
     whole(send2, recv2, s2, r2).wait_send()
@@ -354,62 +342,20 @@
         copy.wait_send()
     for k, copy in passed:
         copy.wait_send()
-    for i, c in enumerate(order):
-        every_rel[c].wait_send()
-        band_copy(sums.at[c, 0], sums.at[c, 0], s_x.at[c], r_x.at[c], up_x).wait_send()
-        band_copy(ahead.at[c], ahead.at[c], s_x2.at[c], r_x.at[c], up_x).wait_send()
+    for c in order:
+        every_x[c].wait_send()
         every_z[c].wait_send()
         all_z[c].wait_send()
-        for copy in gx[i]:
-            copy.wait_send()
-        fw[i].wait_send()
-    stu_copy.wait()
-    grad_copy.wait()
-    for copy in sums_copies:
-        copy.wait()
-
-
-def finish_kernel(
-    factor, sums, mixing, expand, readout, stu_in, grad_in,
-    up_out, down_out, dec_out, gain_out, stu_out, grad_out,
-    up, down, dec, stu, grad, sems,
-):
-    chunks, pieces, depth, wide = sums.shape
-    rows = pieces * depth
-    lat = expand.shape[1]
-    channels = readout.shape[0]
-    ins = [
-        pltpu.make_async_copy(stu_in, stu, sems.at[0]),
-        pltpu.make_async_copy(grad_in, grad, sems.at[1]),
-    ]
-    for copy in ins:
+        all_x[c].wait_send()
+
+
+def write_kernel(*refs):
+    sems = refs[-1]
+    count = len(refs) // 2
+    copies = [pltpu.make_async_copy(refs[k], refs[count + k], sems.at[k]) for k in range(count)]
+    for copy in copies:
         copy.start()
-    low = sums[chunks - 1].astype(F32).reshape(rows, wide)
-    outs = []
-
-    def send(src, dst):
-        outs.append(pltpu.make_async_copy(src, dst, sems.at[2 + len(outs)]))
-        outs[-1].start()
-
-    for c in range(chunks - 1):
-        up[:, c * wide : (c + 1) * wide] = sums[c].astype(F32).reshape(rows, wide) * factor
-    send(up, up_out)
-    read_rows = pad_rows(readout[...].astype(F32), PAD).astype(BF)
-    down[...] = dot(low[:, PAD:].astype(BF), read_rows) * factor
-    send(down, down_out)
-    dec[...] = low[:, :PAD].T[:channels] * factor
-    send(dec, dec_out)
-    for copy in ins:
-        copy.wait()
-    send(stu, stu_out)
-    send(grad, grad_out)
-    terms = up[...] * expand[...].astype(F32)
-    high = terms.astype(BF)
-    rest = (terms - high.astype(F32)).astype(BF)
-    ones = jnp.ones((8, lat), BF)
-    gain = dot(ones, high, 1, 1) + dot(ones, rest, 1, 1)
-    gain_out[...] = gain[:1] / mixing[...]
-    for copy in outs:
+    for copy in copies:
         copy.wait()
 
 
@@ -430,9 +376,8 @@
     lat, hid = expand.shape
     chunks = (hid + 2 * PAD) // CHUNK
     vmem = pl.BlockSpec(memory_space=pltpu.VMEM)
-    anywhere = pl.BlockSpec(memory_space=pl.ANY)
+    hbm = pl.BlockSpec(memory_space=pltpu.HBM)
     quarter = (nz, lat // bands, CHUNK)
-    half = (nz // 2, lat // bands, CHUNK)
     dma = pltpu.SemaphoreType.DMA
     mixing_row = mixing[None]
     read_t = readout.T
@@ -441,20 +386,23 @@
         enc_send[0].T, field, noise[0], lift, enc_recv[0].T, dec_send[0].T, dec_recv[0].T,
         mixing_row, expand, contract, read_t, target[0], weight,
     )
-    student, grad, sums = pl.pallas_call(
-        step_kernel,
+    factor = 1.0 / math.sqrt(bands * nodes)
+    results = pl.pallas_call(
+        functools.partial(step_kernel, factor),
         out_shape=(
-            jax.ShapeDtypeStruct((channels, cells), F32),
-            jax.ShapeDtypeStruct((nodes, lat), BF),
-            jax.ShapeDtypeStruct((chunks, NX, *quarter), BF),
+            pltpu.VMEM((channels, cells), F32),
+            pltpu.VMEM((nodes, lat), BF),
+            pltpu.VMEM((lat, hid), F32),
+            pltpu.VMEM((hid, lat), F32),
+            pltpu.VMEM((channels, lat), F32),
+            pltpu.VMEM((1, lat), F32),
         ),
-        in_specs=[anywhere] * len(ins),
-        out_specs=(anywhere, anywhere, anywhere),
+        in_specs=[hbm] * len(ins),
+        out_specs=(vmem,) * 6,
         scratch_shapes=[pltpu.VMEM(a.shape, a.dtype) for a in ins]
         + [slot_buffer] * 6
         + [
             pltpu.VMEM((members, channels, cells), BF),
-            pltpu.VMEM((channels, cells), F32),
             pltpu.VMEM((members, channels, cells), F32),
             pltpu.VMEM((nodes, slots), BF),
             pltpu.VMEM((slots, nodes), BF),
@@ -468,11 +416,8 @@
             pltpu.VMEM((nodes, lat), F32),
             pltpu.VMEM((nodes, hid), F32),
             pltpu.VMEM((nodes, hid), F32),
-            pltpu.VMEM((nodes, lat), BF),
             pltpu.VMEM((chunks, NX, *quarter), BF),
-            pltpu.VMEM((chunks, 2, *half), BF),
-            pltpu.VMEM((chunks, 2, *half), BF),
-            pltpu.VMEM((chunks, 2, *quarter), BF),
+            pltpu.VMEM((chunks, NX - 1, *quarter), BF),
             pltpu.VMEM((chunks, *quarter), BF),
             pltpu.VMEM((chunks, *quarter), BF),
             pltpu.VMEM((chunks, NX, *quarter), BF),
@@ -480,33 +425,20 @@
         + [dma((len(ins),))]
         + [dma(())] * 8
         + [dma((members // 2,))] * 4
-        + [dma((chunks,))] * 9
-        + [dma((chunks, 2))] * 2
-        + [dma((chunks,))] * 2
-        + [dma(()), dma(()), dma((chunks,))],
+        + [dma((chunks,))] * 8,
         compiler_params=pltpu.CompilerParams(
-            collective_id=0, has_side_effects=True, vmem_limit_bytes=60 << 20
+            collective_id=0, has_side_effects=True, vmem_limit_bytes=40 << 20
         ),
         name="step",
-    )(*ins)
-    factor = 1.0 / math.sqrt(bands * nodes)
-    outs = (
-        jax.ShapeDtypeStruct((lat, hid), F32),
-        jax.ShapeDtypeStruct((hid, lat), F32),
-        jax.ShapeDtypeStruct((channels, lat), F32),
-        jax.ShapeDtypeStruct((1, lat), F32),
-        jax.ShapeDtypeStruct((channels, cells), F32),
-        jax.ShapeDtypeStruct((nodes, lat), BF),
-    )
-    up, down, dec, gain, student, grad = pl.pallas_call(
-        functools.partial(finish_kernel, factor),
-        out_shape=outs,
-        in_specs=[vmem] * 4 + [anywhere] * 2,
-        out_specs=(anywhere, anywhere, anywhere, vmem, anywhere, anywhere),
-        scratch_shapes=[pltpu.VMEM(outs[i].shape, outs[i].dtype) for i in (0, 1, 2, 4, 5)]
-        + [dma((7,))],
-        name="finish",
-    )(sums.reshape(chunks, bands, lat // bands, CHUNK), mixing_row, expand, read_t, student, grad)
+    )(*(pltpu.with_memory_space_constraint(a, pltpu.HBM) for a in ins))
+    student, grad, up, down, dec, gain = pl.pallas_call(
+        write_kernel,
+        out_shape=tuple(jax.ShapeDtypeStruct(a.shape, a.dtype) for a in results),
+        in_specs=[vmem] * 6,
+        out_specs=(hbm,) * 6,
+        scratch_shapes=[dma((6,))],
+        name="write",
+    )(*(pltpu.with_memory_space_constraint(a, pltpu.VMEM) for a in results))
     return student[None], grad[None], up[None], down[None], dec.T[None], gain
 
 

time: 95 us -> 88.5 us (0.932)
  the two profiles are of different devices: /device:TPU:4 before, /device:TPU:1 now
where the time goes in v3:
time: 88.5 us; the launch traced here: 88.4 us
  Pallas kernels  87.8 us (99%)
    pallas_call x1, Pallas kernels, body(): pl.pallas_call(functools.partial(step_kernel, factor), out_shape=(pltpu.V...  86.2 us

profile of v3, /device:TPU:1, one launch (start us, length us, event | category | flops | bytes accessed | tf_op | source)
XLA Modules:
  0.0 88.4 jit_solution(3569231807906960484)
XLA Ops:
  0.6 86.2 %step.1 = (f32[80,256]{1,0:T(8,128)S(1)}, bf16[256,512]{1,0:T(8,128)(2,1)S(1)}, f32[512,512]{1,0:T(8,128)S(1)}, f32[512,512]{1,0:T(8,128)S(1)}, f32[80,512]{1,0:T(8,128)S(1)}, /*index=5*/f32[1,512]{1,0:T(1,128)S(1)}) custom-call(s32[8,64]{1,0:T(8,128)} %bitcast.26, f32[80,256]{1,0:T(8,128)} %field_in.1, bf16[80,256]{1,0:T(8,128)(2,1)} %bitcast.24, ...), custom_call_target="tpu_custom_call" | custom-call | tf_op jit(solution)/shard_map/step/pallas_call | solution.py:390
  86.9 1.5 %write.1 = (f32[80,256]{1,0:T(8,128)}, bf16[256,512]{1,0:T(8,128)(2,1)}, f32[512,512]{1,0:T(8,128)}, f32[512,512]{1,0:T(8,128)}, f32[80,512]{1,0:T(8,128)}, /*index=5*/f32[1,512]{1,0:T(1,128)}) custom-call(f32[80,256]{1,0:T(8,128)S(1)} %get-tuple-element.18.refs_0_, bf16[256,512]{1,0:T(8,128)(2,1)S(1)} %get-tuple-element.19.refs_1_, ...), custom_call_target="tpu_custom_call" | custom-call | tf_op jit(solution)/shard_map/write/pallas_call | solution.py:434

commit v4 on v3

--- a/solution.py
+++ b/solution.py
@@ -13,6 +13,7 @@
 F32 = jnp.float32
 NX = 4
 PAD = 128
+CHUNKS = (("down", 0, 128), ("dec", 0, 128), ("up", 0, 128), ("up", 128, 128), ("up", 256, 128), ("up", 384, 128))
 smooth_sq = 0.01
 norm_eps = 1e-05
 
@@ -23,6 +24,10 @@
 
 def slope(diff):
     return diff * lax.rsqrt(diff * diff + smooth_sq)
+
+
+def sigmoid(v):
+    return 0.5 + 0.5 * jnp.tanh(0.5 * v)
 
 
 def pad_rows(a, rows):
@@ -56,17 +61,17 @@
     enc_send, field, noise, lift, enc_recv, dec_send, dec_recv,
     mixing, expand, contract, readout, target, weight,
     send1, recv1, send2, recv2, send3, recv3,
-    teach, stus, enc_land, dec_pick, dec_land, fill, readp, both,
+    teach, halves_b, halves, stus, weights, inverses, pieces, enc_land, dec_pick, dec_land, fill, readp, both,
     normed_t, hidden_t, next_t, state, hidden_pre, dsilu,
-    sums, from_x, part, from_z, full,
-    loads, s1, r1, s2, r2, s3, r3, st, rt, ss, rs, sf, rf,
-    s_x, r_x, s_z, r_z, s_gz, r_gz, s_gx, r_gx,
+    loads, s1, r1, s2, r2, s3, r3, st, rt, ss, rs, sp, rp,
+    s_x, r_x, s_z, r_z, s_gz, r_gz, s_gx, r_gx, *chunk_refs,
 ):
     bands = send1.shape[0]
     members = teach.shape[0]
     nz = bands // NX
     half = nz // 2
-    chunks = sums.shape[0]
+    chunks = len(CHUNKS)
+    sums, from_x, part, from_z, full = (chunk_refs[k * chunks : (k + 1) * chunks] for k in range(5))
     b = lax.axis_index("band")
     m = lax.axis_index("member")
     z = b // NX
@@ -76,6 +81,7 @@
     slots = send1.shape[0] * send1.shape[1]
     channels, cells = field.shape
     nodes = cells
+    cut = cells // 2
 
     into = (
         enc_send, field, noise, lift, enc_recv, dec_send, dec_recv,
@@ -140,6 +146,9 @@
         some = pl.ds(0, bands - 1)
         return band_copy(send.at[some], recv.at[some], ssem, rsem, (b + 1) % bands)
 
+    def fill_at(h):
+        return fill[:, pl.ds(pl.multiple_of(h * cut, cut), cut)]
+
     for copy in load[:3]:
         copy.wait()
     inputs = pad_rows((field[...] + noise[...].astype(F32)).astype(BF).astype(F32), PAD).astype(BF)
@@ -149,12 +158,21 @@
     for copy in load[3:]:
         copy.wait()
 
-    def send_target(k, carry):
-        member_copy(target, teach.at[m], st, rt, (m + k) % members).start()
-        return carry
-
-    lax.fori_loop(1, members, send_target, 0)
-    teach[pl.ds(m, 1)] = target[...][None]
+    chips = members // 2
+    partner = y * 2 + 1 - core
+    for h in range(2):
+        halves_b[h] = target[:, h * cut : (h + 1) * cut]
+        weights[h] = weight[:, h * cut : (h + 1) * cut].astype(F32)
+
+    def shared(src, dst, ssem, rsem):
+        for k in (2, 1, 3):
+            for c in range(2):
+                to = ((y + k) % chips) * 2 + c
+                member_copy(src.at[c], dst.at[m], ssem, rsem, to).start()
+        member_copy(src.at[1 - core], dst.at[m], ssem, rsem, partner).start()
+        dst[pl.ds(m, 1)] = src[pl.ds(core, 1)]
+
+    shared(halves_b, teach, st, rt)
 
     land = one_hot(enc_recv, nodes).T
     enc_land[...] = land.astype(BF)
@@ -168,14 +186,18 @@
     cover = one_hot(dec_recv, cells)
     fill[...] = cover.astype(BF)
     inverse = 1.0 / jnp.maximum(jnp.sum(cover, axis=0, keepdims=True), 1.0)
+    for h in range(2):
+        inverses[h] = inverse[:, h * cut : (h + 1) * cut]
 
     whole(send1, recv1, s1, r1).wait_recv()
-    rows = jax.nn.silu(dot(from_slots(recv1), lift_rows)).astype(BF)
+    embedded = dot(from_slots(recv1), lift_rows)
+    rows = (embedded * sigmoid(embedded)).astype(BF)
     state[...] = dot(enc_land[...], rows) * edge_scale
     recip = lax.rsqrt(jnp.mean(state[...] * state[...], axis=1, keepdims=True) + norm_eps)
     normed = (state[...] * recip * mixing[...]).astype(BF)
     hidden_pre[...] = dot(normed, expand[...])
-    hidden = jax.nn.silu(hidden_pre[...]).astype(BF)
+    gate = sigmoid(hidden_pre[...])
+    hidden = (hidden_pre[...] * gate).astype(BF)
     next_b = (state[...] + dot(hidden, contract[...])).astype(BF)
     projected = dot(next_b, readp[...], 1, 1).astype(BF)
     to_slots(dot(dec_pick[...], projected), send2)
@@ -184,8 +206,7 @@
     normed_t[...] = normed.astype(F32).T.astype(BF)
     hidden_t[...] = hidden.astype(F32).T.astype(BF)
     next_t[...] = next_b.astype(F32).T.astype(BF)
-    sigma = jax.nn.sigmoid(hidden_pre[...])
-    dsilu[...] = sigma * (1.0 + hidden_pre[...] * (1.0 - sigma))
+    dsilu[...] = gate * (1.0 + hidden_pre[...] * (1.0 - gate))
 
     seven = pl.ds(0, members - 1)
     every_target = member_copy(teach.at[seven], teach.at[seven], st, rt, (m + 1) % members)
@@ -195,87 +216,73 @@
     mine = field[...] + grid_sum * inverse
     stu[...] = mine
 
-    chips = members // 2
-    partner = y * 2 + 1 - core
-
-    def chip(k):
-        return ((y + k) % chips) * 2
-
-    direct = [
-        member_copy(stu, stus.at[m], ss.at[k], rs.at[k], chip(k) + core if k else partner)
-        for k in range(chips)
-    ]
-    for k in (2, 1, 3, 0):
-        direct[k].start()
-    pull = jnp.zeros((channels, cells), F32)
+    for h in range(2):
+        halves[h] = mine[:, h * cut : (h + 1) * cut]
+    shared(halves, stus, ss, rs)
+    stu[...] = mine
+    every_student = member_copy(stus.at[seven], stus.at[seven], ss, rs, (m + 1) % members)
+    every_student.wait_recv()
+    both_mine = stus[pl.ds(y * 2, 2)]
+    pull = jnp.zeros(both_mine.shape, F32)
     for j in range(members):
-        pull = pull + slope(mine - teach[j].astype(F32))
-    passed = []
-    for k in (0, 1, 3, 2):
-        direct[k].wait_recv()
-        if k:
-            source = chip(chips - k) + core
-            copy = member_copy(stus.at[source], stus.at[source], sf.at[k], rf.at[k], partner)
-            copy.start()
-            passed.append((k, copy))
-        else:
-            source = partner
-        pull = pull - slope(mine - stus[pl.ds(source, 1)][0])
-    for k, copy in passed:
-        copy.wait_recv()
-        pull = pull - slope(mine - stus[pl.ds(chip(chips - k) + 1 - core, 1)][0])
-    scaled = weight[...].astype(F32) * pull * inverse
-    to_slots(dot(fill[...], pad_rows(scaled, PAD).astype(BF), 1, 1), send3)
+        pull = pull + (slope(both_mine - teach[j].astype(F32)) - slope(both_mine - stus[j]))
+    pull = pull * (weights[pl.ds(core, 1)] * inverses[pl.ds(core, 1)])
+    pieces[pl.ds(0, 2)] = pull.astype(BF)
+    pass_on = member_copy(pieces.at[1 - core], pieces.at[2], sp, rp, partner)
+    pass_on.start()
+    first = pad_rows(pieces[pl.ds(core, 1)][0].astype(F32), PAD).astype(BF)
+    picked = dot(fill_at(core), first, 1, 1)
+    pass_on.wait_recv()
+    second = pad_rows(pieces[2].astype(F32), PAD).astype(BF)
+    to_slots(picked + dot(fill_at(1 - core), second, 1, 1), send3)
     exchange(send3, recv3, s3, r3)
     whole(send3, recv3, s3, r3).wait_recv()
 
     node_grad = dot(dec_land[...], from_slots(recv3)).astype(BF)
-    quarter = sums.shape[1:4]
-    wide = sums.shape[4]
+    blocks = sums[0].shape[:3]
     three = pl.ds(0, NX - 1)
     next_x = z * NX + (x + 1) % NX
     far_x = (2, 1, 3)
 
-    def launch(c):
+    pre = None
+    for c, (kind, at, width) in enumerate(CHUNKS):
+        if kind == "down":
+            value = dot(hidden_t[...], node_grad)
+        elif kind == "dec":
+            value = dot(next_t[...], node_grad)
+        else:
+            if pre is None:
+                pre = (dot(node_grad, both[...], 1, 1) * dsilu[...]).astype(BF)
+            value = dot(normed_t[...], pre[:, at : at + width])
+        sums[c][...] = value.reshape(*blocks, width).astype(BF)
         for k in far_x:
             to = (x + k) % NX
             band_copy(
-                sums.at[c, to], from_x.at[c, k - 1], s_x.at[c], r_x.at[c], z * NX + to
+                sums[c].at[to], from_x[c].at[k - 1], s_x.at[c], r_x.at[c], z * NX + to
             ).start()
 
-    last = chunks - 1
-    sums[last, :, :, :, :PAD] = dot(next_t[...], node_grad).reshape(*quarter, PAD).astype(BF)
-    sums[last, :, :, :, PAD:] = dot(hidden_t[...], node_grad).reshape(*quarter, PAD).astype(BF)
-    launch(last)
-    pre = (dot(node_grad, both[...], 1, 1) * dsilu[...]).astype(BF)
-    for c in range(last):
-        some = pre[:, c * wide : (c + 1) * wide]
-        sums[c] = dot(normed_t[...], some).reshape(*quarter, wide).astype(BF)
-        launch(c)
-
-    order = [last, *range(last)]
     every_x = [
-        band_copy(sums.at[c, three], from_x.at[c], s_x.at[c], r_x.at[c], next_x)
+        band_copy(sums[c].at[three], from_x[c], s_x.at[c], r_x.at[c], next_x)
         for c in range(chunks)
     ]
     ring = pl.ds(0, nz - 1)
     next_z = ((z + 1) % nz) * NX + x
-    for c in order:
+    for c in range(chunks):
         every_x[c].wait_recv()
-        total = sums[c, pl.ds(x, 1)][0].astype(F32)
+        total = sums[c][pl.ds(x, 1)][0].astype(F32)
         for k in range(NX - 1):
-            total = total + from_x[c, k].astype(F32)
-        part[c] = total.astype(BF)
+            total = total + from_x[c][k].astype(F32)
+        part[c][...] = total.astype(BF)
 
         def send_z(j, carry, c=c):
             to = (z + far_first(j, half)) % nz
             band_copy(
-                part.at[c, to], from_z.at[c, z], s_z.at[c], r_z.at[c], to * NX + x
+                part[c].at[to], from_z[c].at[z], s_z.at[c], r_z.at[c], to * NX + x
             ).start()
             return carry
 
         lax.fori_loop(0, nz - 1, send_z, 0)
-        from_z[c, pl.ds(z, 1)] = part[c, pl.ds(z, 1)]
+        from_z[c][pl.ds(z, 1)] = part[c][pl.ds(z, 1)]
 
     next_grad = dot(node_grad, readp[...])
     gained = dot(pre, expand[...], 1, 1) * mixing[...]
@@ -285,52 +292,52 @@
     ).astype(BF)
 
     every_z = [
-        band_copy(from_z.at[c, ring], from_z.at[c, ring], s_z.at[c], r_z.at[c], next_z)
+        band_copy(from_z[c].at[ring], from_z[c].at[ring], s_z.at[c], r_z.at[c], next_z)
         for c in range(chunks)
     ]
     all_z = [
-        band_copy(full.at[c, x, ring], full.at[c, x, ring], s_gz.at[c], r_gz.at[c], next_z)
+        band_copy(full[c].at[x, ring], full[c].at[x, ring], s_gz.at[c], r_gz.at[c], next_z)
         for c in range(chunks)
     ]
-    for c in order:
+    all_x = [
+        band_copy(full[c].at[three], full[c].at[three], s_gx.at[c], r_gx.at[c], next_x)
+        for c in range(chunks)
+    ]
+    for c in range(chunks):
         every_z[c].wait_recv()
-        piece = jnp.sum(from_z[c].astype(F32), axis=0).astype(BF)
-        full[c, pl.ds(x, 1), pl.ds(z, 1)] = piece[None, None]
+        piece = jnp.sum(from_z[c][...].astype(F32), axis=0).astype(BF)
+        full[c][pl.ds(x, 1), pl.ds(z, 1)] = piece[None, None]
 
         def gather_z(j, carry, c=c):
             to = (z + far_first(j, half)) % nz
-            mine_z = full.at[c, x, z]
+            mine_z = full[c].at[x, z]
             band_copy(mine_z, mine_z, s_gz.at[c], r_gz.at[c], to * NX + x).start()
             return carry
 
         lax.fori_loop(0, nz - 1, gather_z, 0)
 
-    all_x = [
-        band_copy(full.at[c, three], full.at[c, three], s_gx.at[c], r_gx.at[c], next_x)
-        for c in range(chunks)
-    ]
-    for c in order:
+    for c in range(chunks):
         all_z[c].wait_recv()
+        mine_x = full[c].at[x]
         for k in far_x:
-            mine_x = full.at[c, x]
             band_copy(mine_x, mine_x, s_gx.at[c], r_gx.at[c], z * NX + (x + k) % NX).start()
 
-    rows = quarter[0] * quarter[1] * quarter[2]
-    ones = jnp.ones((8, wide), BF)
+    rows = blocks[0] * blocks[1] * blocks[2]
     gain = jnp.zeros((8, rows), F32)
-    for c in order:
+    for c, (kind, at, width) in enumerate(CHUNKS):
         all_x[c].wait_recv()
-        some = full[c].astype(F32).reshape(rows, wide)
-        if c == last:
-            down_out[...] = dot(some[:, PAD:].astype(BF), readp[...]) * factor
-            dec_out[...] = some[:, :PAD].T[:channels] * factor
+        some = full[c][...].astype(F32).reshape(rows, width)
+        if kind == "down":
+            down_out[...] = dot(some.astype(BF), readp[...]) * factor
+        elif kind == "dec":
+            dec_out[...] = some.T[:channels] * factor
         else:
-            at = slice(c * wide, (c + 1) * wide)
             some = some * factor
-            up_out[:, at] = some
-            terms = some * expand[:, at].astype(F32)
+            up_out[:, at : at + width] = some
+            terms = some * expand[:, at : at + width].astype(F32)
             main = terms.astype(BF)
             rest = (terms - main.astype(F32)).astype(BF)
+            ones = jnp.ones((8, width), BF)
             gain = gain + dot(ones, main, 1, 1) + dot(ones, rest, 1, 1)
     gain_out[...] = gain[:1] / mixing[...]
 
@@ -338,11 +345,9 @@
     whole(send2, recv2, s2, r2).wait_send()
     whole(send3, recv3, s3, r3).wait_send()
     every_target.wait_send()
-    for copy in direct:
-        copy.wait_send()
-    for k, copy in passed:
-        copy.wait_send()
-    for c in order:
+    every_student.wait_send()
+    pass_on.wait_send()
+    for c in range(chunks):
         every_x[c].wait_send()
         every_z[c].wait_send()
         all_z[c].wait_send()
@@ -357,9 +362,6 @@
         copy.start()
     for copy in copies:
         copy.wait()
-
-
-CHUNK = 256
 
 
 def body(
@@ -374,10 +376,15 @@
     cap = enc_send.shape[2]
     slots = bands * cap
     lat, hid = expand.shape
-    chunks = (hid + 2 * PAD) // CHUNK
+    chunks = len(CHUNKS)
     vmem = pl.BlockSpec(memory_space=pltpu.VMEM)
     hbm = pl.BlockSpec(memory_space=pltpu.HBM)
-    quarter = (nz, lat // bands, CHUNK)
+    cut = cells // 2
+    block = (nz, lat // bands)
+
+    def per_chunk(*lead):
+        return [pltpu.VMEM((*lead, *block, width), BF) for _, _, width in CHUNKS]
+
     dma = pltpu.SemaphoreType.DMA
     mixing_row = mixing[None]
     read_t = readout.T
@@ -402,8 +409,13 @@
         scratch_shapes=[pltpu.VMEM(a.shape, a.dtype) for a in ins]
         + [slot_buffer] * 6
         + [
-            pltpu.VMEM((members, channels, cells), BF),
-            pltpu.VMEM((members, channels, cells), F32),
+            pltpu.VMEM((members, channels, cut), BF),
+            pltpu.VMEM((2, channels, cut), BF),
+            pltpu.VMEM((2, channels, cut), F32),
+            pltpu.VMEM((members, channels, cut), F32),
+            pltpu.VMEM((2, channels, cut), F32),
+            pltpu.VMEM((2, 1, cut), F32),
+            pltpu.VMEM((3, channels, cut), BF),
             pltpu.VMEM((nodes, slots), BF),
             pltpu.VMEM((slots, nodes), BF),
             pltpu.VMEM((nodes, slots), BF),
@@ -416,16 +428,15 @@
             pltpu.VMEM((nodes, lat), F32),
             pltpu.VMEM((nodes, hid), F32),
             pltpu.VMEM((nodes, hid), F32),
-            pltpu.VMEM((chunks, NX, *quarter), BF),
-            pltpu.VMEM((chunks, NX - 1, *quarter), BF),
-            pltpu.VMEM((chunks, *quarter), BF),
-            pltpu.VMEM((chunks, *quarter), BF),
-            pltpu.VMEM((chunks, NX, *quarter), BF),
         ]
         + [dma((len(ins),))]
-        + [dma(())] * 8
-        + [dma((members // 2,))] * 4
-        + [dma((chunks,))] * 8,
+        + [dma(())] * 12
+        + [dma((chunks,))] * 8
+        + per_chunk(NX)
+        + per_chunk(NX - 1)
+        + per_chunk()
+        + per_chunk()
+        + per_chunk(NX),
         compiler_params=pltpu.CompilerParams(
             collective_id=0, has_side_effects=True, vmem_limit_bytes=40 << 20
         ),

time: 88.5 us -> 87.3 us (0.986)
  Pallas kernels: 87.8 us -> 86.1 us
    pallas_call x1, Pallas kernels: 86.2 us -> 84.5 us  [body(): pl.pallas_call(functools.partial(step_kernel, factor), out_shape=(pltpu.V...]
where the time goes in v4:
time: 87.3 us; the launch traced here: 86.7 us
  Pallas kernels  86.1 us (99%)
    pallas_call x1, Pallas kernels, body(): pl.pallas_call(functools.partial(step_kernel, factor), out_shape=(pltpu.V...  84.5 us

profile of v4, /device:TPU:1, one launch (start us, length us, event | category | flops | bytes accessed | tf_op | source)
XLA Modules:
  0.0 86.7 jit_solution(507325115527633506)
XLA Ops:
  0.6 84.5 %step.1 = (f32[80,256]{1,0:T(8,128)S(1)}, bf16[256,512]{1,0:T(8,128)(2,1)S(1)}, f32[512,512]{1,0:T(8,128)S(1)}, f32[512,512]{1,0:T(8,128)S(1)}, f32[80,512]{1,0:T(8,128)S(1)}, /*index=5*/f32[1,512]{1,0:T(1,128)S(1)}) custom-call(s32[8,64]{1,0:T(8,128)} %bitcast.26, f32[80,256]{1,0:T(8,128)} %field_in.1, bf16[80,256]{1,0:T(8,128)(2,1)} %bitcast.24, ...), custom_call_target="tpu_custom_call" | custom-call | tf_op jit(solution)/shard_map/step/pallas_call | solution.py:397
  85.2 1.5 %write.1 = (f32[80,256]{1,0:T(8,128)}, bf16[256,512]{1,0:T(8,128)(2,1)}, f32[512,512]{1,0:T(8,128)}, f32[512,512]{1,0:T(8,128)}, f32[80,512]{1,0:T(8,128)}, /*index=5*/f32[1,512]{1,0:T(1,128)}) custom-call(f32[80,256]{1,0:T(8,128)S(1)} %get-tuple-element.18.refs_0_, bf16[256,512]{1,0:T(8,128)(2,1)S(1)} %get-tuple-element.19.refs_1_, ...), custom_call_target="tpu_custom_call" | custom-call | tf_op jit(solution)/shard_map/write/pallas_call | solution.py:445

commit v5 on v4

--- a/solution.py
+++ b/solution.py
@@ -61,9 +61,9 @@
     enc_send, field, noise, lift, enc_recv, dec_send, dec_recv,
     mixing, expand, contract, readout, target, weight,
     send1, recv1, send2, recv2, send3, recv3,
-    teach, halves_b, halves, stus, weights, inverses, pieces, enc_land, dec_pick, dec_land, fill, readp, both,
+    teach, halves_b, halves, stus, weights, inverses, pulls, pieces, enc_land, dec_pick, dec_land, fill, readp, both,
     normed_t, hidden_t, next_t, state, hidden_pre, dsilu,
-    loads, s1, r1, s2, r2, s3, r3, st, rt, ss, rs, sp, rp,
+    loads, s1, r1, s2, r2, s3, r3, st, rt, pt, ss, rs, ps, sp, rp,
     s_x, r_x, s_z, r_z, s_gz, r_gz, s_gx, r_gx, *chunk_refs,
 ):
     bands = send1.shape[0]
@@ -96,7 +96,9 @@
         copy.start()
 
     def peer_of(t):
-        return ((z + far_first(t // NX, half)) % nz) * NX + (x + NX - 1 - t % NX) % NX
+        k = t % NX
+        step = (1 - k // 2) * (2 + k) + (k // 2) * (3 - k)
+        return ((z + far_first(t // NX, half)) % nz) * NX + (x + step) % NX
 
     barrier = pltpu.get_barrier_semaphore()
 
@@ -164,15 +166,17 @@
         halves_b[h] = target[:, h * cut : (h + 1) * cut]
         weights[h] = weight[:, h * cut : (h + 1) * cut].astype(F32)
 
-    def shared(src, dst, ssem, rsem):
+    def shared(src, dst, ssem, rsem, psem):
         for k in (2, 1, 3):
             for c in range(2):
                 to = ((y + k) % chips) * 2 + c
                 member_copy(src.at[c], dst.at[m], ssem, rsem, to).start()
-        member_copy(src.at[1 - core], dst.at[m], ssem, rsem, partner).start()
+        near = member_copy(src.at[1 - core], dst.at[m], ssem, psem, partner)
+        near.start()
         dst[pl.ds(m, 1)] = src[pl.ds(core, 1)]
-
-    shared(halves_b, teach, st, rt)
+        return near
+
+    near_target = shared(halves_b, teach, st, rt, pt)
 
     land = one_hot(enc_recv, nodes).T
     enc_land[...] = land.astype(BF)
@@ -209,8 +213,10 @@
     dsilu[...] = gate * (1.0 + hidden_pre[...] * (1.0 - gate))
 
     seven = pl.ds(0, members - 1)
+    six = pl.ds(0, members - 2)
     every_target = member_copy(teach.at[seven], teach.at[seven], st, rt, (m + 1) % members)
-    every_target.wait_recv()
+    member_copy(teach.at[six], teach.at[six], st, rt, (m + 1) % members).wait_recv()
+    near_target.wait_recv()
     whole(send2, recv2, s2, r2).wait_recv()
     grid_sum = dot(from_slots(recv2), fill[...], 0, 0)[:channels]
     mine = field[...] + grid_sum * inverse
@@ -218,14 +224,19 @@
 
     for h in range(2):
         halves[h] = mine[:, h * cut : (h + 1) * cut]
-    shared(halves, stus, ss, rs)
+    near_student = shared(halves, stus, ss, rs, ps)
     stu[...] = mine
     every_student = member_copy(stus.at[seven], stus.at[seven], ss, rs, (m + 1) % members)
-    every_student.wait_recv()
+    near_student.wait_recv()
     both_mine = stus[pl.ds(y * 2, 2)]
     pull = jnp.zeros(both_mine.shape, F32)
     for j in range(members):
-        pull = pull + (slope(both_mine - teach[j].astype(F32)) - slope(both_mine - stus[j]))
+        pull = pull + slope(both_mine - teach[j].astype(F32))
+    pulls[...] = pull
+    member_copy(stus.at[six], stus.at[six], ss, rs, (m + 1) % members).wait_recv()
+    pull = pulls[...]
+    for j in range(members):
+        pull = pull - slope(both_mine - stus[j])
     pull = pull * (weights[pl.ds(core, 1)] * inverses[pl.ds(core, 1)])
     pieces[pl.ds(0, 2)] = pull.astype(BF)
     pass_on = member_copy(pieces.at[1 - core], pieces.at[2], sp, rp, partner)
@@ -415,6 +426,7 @@
             pltpu.VMEM((members, channels, cut), F32),
             pltpu.VMEM((2, channels, cut), F32),
             pltpu.VMEM((2, 1, cut), F32),
+            pltpu.VMEM((2, channels, cut), F32),
             pltpu.VMEM((3, channels, cut), BF),
             pltpu.VMEM((nodes, slots), BF),
             pltpu.VMEM((slots, nodes), BF),
@@ -430,7 +442,7 @@
             pltpu.VMEM((nodes, hid), F32),
         ]
         + [dma((len(ins),))]
-        + [dma(())] * 12
+        + [dma(())] * 14
         + [dma((chunks,))] * 8
         + per_chunk(NX)
         + per_chunk(NX - 1)

time: 87.3 us -> 86.6 us (level)
  Pallas kernels: 86.1 us -> 84.5 us
    pallas_call x1, Pallas kernels: 84.5 us -> 83 us  [body(): pl.pallas_call(functools.partial(step_kernel, factor), out_shape=(pltpu.V...]
where the time goes in v5:
time: 86.6 us; the launch traced here: 85.2 us
  Pallas kernels  84.5 us (98%)
    pallas_call x1, Pallas kernels, body(): pl.pallas_call(functools.partial(step_kernel, factor), out_shape=(pltpu.V...  83 us

profile of v5, /device:TPU:1, one launch (start us, length us, event | category | flops | bytes accessed | tf_op | source)
XLA Modules:
  0.0 85.2 jit_solution(3211043898013313887)
XLA Ops:
  0.6 83.0 %step.1 = (f32[80,256]{1,0:T(8,128)S(1)}, bf16[256,512]{1,0:T(8,128)(2,1)S(1)}, f32[512,512]{1,0:T(8,128)S(1)}, f32[512,512]{1,0:T(8,128)S(1)}, f32[80,512]{1,0:T(8,128)S(1)}, /*index=5*/f32[1,512]{1,0:T(1,128)S(1)}) custom-call(s32[8,64]{1,0:T(8,128)} %bitcast.26, f32[80,256]{1,0:T(8,128)} %field_in.1, bf16[80,256]{1,0:T(8,128)(2,1)} %bitcast.24, ...), custom_call_target="tpu_custom_call" | custom-call | tf_op jit(solution)/shard_map/step/pallas_call | solution.py:408
  83.6 1.5 %write.1 = (f32[80,256]{1,0:T(8,128)}, bf16[256,512]{1,0:T(8,128)(2,1)}, f32[512,512]{1,0:T(8,128)}, f32[512,512]{1,0:T(8,128)}, f32[80,512]{1,0:T(8,128)}, /*index=5*/f32[1,512]{1,0:T(1,128)}) custom-call(f32[80,256]{1,0:T(8,128)S(1)} %get-tuple-element.18.refs_0_, bf16[256,512]{1,0:T(8,128)(2,1)S(1)} %get-tuple-element.19.refs_1_, ...), custom_call_target="tpu_custom_call" | custom-call | tf_op jit(solution)/shard_map/write/pallas_call | solution.py:457

commit v6 on v5

--- a/solution.py
+++ b/solution.py
@@ -264,7 +264,10 @@
         else:
             if pre is None:
                 pre = (dot(node_grad, both[...], 1, 1) * dsilu[...]).astype(BF)
-            value = dot(normed_t[...], pre[:, at : at + width])
+            if at % (2 * width) == 0:
+                two = dot(normed_t[...], pre[:, at : at + 2 * width])
+            first = at % (2 * width)
+            value = two[:, first : first + width]
         sums[c][...] = value.reshape(*blocks, width).astype(BF)
         for k in far_x:
             to = (x + k) % NX
@@ -348,8 +351,8 @@
             terms = some * expand[:, at : at + width].astype(F32)
             main = terms.astype(BF)
             rest = (terms - main.astype(F32)).astype(BF)
-            ones = jnp.ones((8, width), BF)
-            gain = gain + dot(ones, main, 1, 1) + dot(ones, rest, 1, 1)
+            ones = jnp.ones((8, 2 * width), BF)
+            gain = gain + dot(ones, jnp.concatenate([main, rest], axis=1), 1, 1)
     gain_out[...] = gain[:1] / mixing[...]
 
     whole(send1, recv1, s1, r1).wait_send()
@@ -369,8 +372,8 @@
     sems = refs[-1]
     count = len(refs) // 2
     copies = [pltpu.make_async_copy(refs[k], refs[count + k], sems.at[k]) for k in range(count)]
-    for copy in copies:
-        copy.start()
+    for k in sorted(range(count), key=lambda k: -math.prod(refs[k].shape)):
+        copies[k].start()
     for copy in copies:
         copy.wait()
 

time: 86.6 us -> 86.3 us (level)
  no operation moved by 1% of the time
where the time goes in v6:
time: 86.3 us; the launch traced here: 85.5 us
  Pallas kernels  84.9 us (98%)
    pallas_call x1, Pallas kernels, body(): pl.pallas_call(functools.partial(step_kernel, factor), out_shape=(pltpu.V...  83.4 us

profile of v6, /device:TPU:1, one launch (start us, length us, event | category | flops | bytes accessed | tf_op | source)
XLA Modules:
  0.0 85.5 jit_solution(132693433957299959)
XLA Ops:
  0.6 83.4 %step.1 = (f32[80,256]{1,0:T(8,128)S(1)}, bf16[256,512]{1,0:T(8,128)(2,1)S(1)}, f32[512,512]{1,0:T(8,128)S(1)}, f32[512,512]{1,0:T(8,128)S(1)}, f32[80,512]{1,0:T(8,128)S(1)}, /*index=5*/f32[1,512]{1,0:T(1,128)S(1)}) custom-call(s32[8,64]{1,0:T(8,128)} %bitcast.26, f32[80,256]{1,0:T(8,128)} %field_in.1, bf16[80,256]{1,0:T(8,128)(2,1)} %bitcast.24, ...), custom_call_target="tpu_custom_call" | custom-call | tf_op jit(solution)/shard_map/step/pallas_call | solution.py:411
  84.0 1.5 %write.1 = (f32[80,256]{1,0:T(8,128)}, bf16[256,512]{1,0:T(8,128)(2,1)}, f32[512,512]{1,0:T(8,128)}, f32[512,512]{1,0:T(8,128)}, f32[80,512]{1,0:T(8,128)}, /*index=5*/f32[1,512]{1,0:T(1,128)}) custom-call(f32[80,256]{1,0:T(8,128)S(1)} %get-tuple-element.18.refs_0_, bf16[256,512]{1,0:T(8,128)(2,1)S(1)} %get-tuple-element.19.refs_1_, ...), custom_call_target="tpu_custom_call" | custom-call | tf_op jit(solution)/shard_map/write/pallas_call | solution.py:460
